TPU v7x, 32 devices: a whole 2x2x4 slice. The times are simulated.
32 devices in a mesh: colour: 2 (over core), sub: 16 (over z, y, x).
Axes of the slice: x: 2, y: 2, z: 4, core: 2. Of those that a mesh axis runs over, the one named last changes fastest.
Arguments:
- rhs: float32 [3, 64, 256, 512], P(None, 'sub'), may hold values from -60 to 60
- diagonal: float32 [64, 256, 512], P('sub'), may hold values from 0.2 to 6
Outputs:
- solution: float32 [3, 64, 256, 512], P(None, 'sub', None, 'colour')
- residual: float32 [3, 64, 256, 512], P(None, 'sub', None, 'colour')
- norms: float32 [3], replicated
All inputs are finite; a program needn't handle non-finite values.
Results may differ from a plain program's by a relative error of at most 0.0003.
Values sent between devices are 32-bit elements; how exact they have to be, the bound alone decides.
A program may use at most 128 MiB of HBM per device.

v0:
```python
import functools

import jax
import jax.numpy as jnp
from jax import lax
from jax.experimental import pallas as pl
from jax.experimental.pallas import tpu as pltpu
from jax.sharding import PartitionSpec as P

SWEEPS = 8
OMEGA = 0.8
RIM = 2 * SWEEPS
UNROLL = 6
ROWS = 8
LANES = 128


def shift(value, last, axis, step):
    size = value.shape[axis]
    at = lax.broadcasted_iota(jnp.int32, value.shape, axis)
    if step > 0:
        return pltpu.roll(jnp.where(at == size - 1, last, value), 1, axis)
    return pltpu.roll(jnp.where(at == 0, last, value), size - 1, axis)


def lateral(planes, p, t, before, after):
    row = planes[p]
    zero = jnp.zeros_like(row[t])
    low = row[t - 1] if t > 0 else zero
    high = row[t + 1] if t + 1 < len(row) else zero
    total = shift(row[t], before, 0, 1) + shift(row[t], after, 0, -1)
    return total + (shift(row[t], low, 1, 1) + shift(row[t], high, 1, -1))


def lane(t):
    return slice(t * LANES, (t + 1) * LANES)


def solve_kernel(order, extra_ref, resid_ref, scale_ref, lo_ref, hi_ref, sq, ea, eb):
    _, rows, depth = scale_ref.shape
    tiles = depth // LANES
    span = len(order)
    refs = [(extra_ref, 0) if at < 0 else (resid_ref, at) for at in order]
    blank = jnp.zeros((span, ROWS, depth), jnp.float32)
    for buf in (ea, eb):
        buf[:, :ROWS, :] = blank
        buf[:, rows + ROWS :, :] = blank

    def first(j, carry):
        r = pl.multiple_of(j * ROWS, ROWS)
        for p, (ref, at) in enumerate(refs):
            value = scale_ref[p, pl.ds(r, ROWS), :] * ref[at, pl.ds(r, ROWS), :]
            sq[p, pl.ds(r, ROWS), :] = value
            ea[p, pl.ds(r + ROWS, ROWS), :] = value
        return carry

    lax.fori_loop(0, rows // ROWS, first, 0)
    src, dst = ea, eb
    for sweep in range(1, SWEEPS):
        final = sweep == SWEEPS - 1

        def body(j, carry, src=src, dst=dst, final=final):
            r = pl.multiple_of(j * ROWS, ROWS)
            planes = [
                [src[p, pl.ds(r + ROWS, ROWS), lane(t)] for t in range(tiles)] for p in range(span)
            ]
            for p in range(span):
                for t in range(tiles):
                    beside = lateral(
                        planes,
                        p,
                        t,
                        src[p, pl.ds(r, ROWS), lane(t)],
                        src[p, pl.ds(r + 2 * ROWS, ROWS), lane(t)],
                    )
                    if p > 0:
                        beside = beside + planes[p - 1][t]
                    if p + 1 < span:
                        beside = beside + planes[p + 1][t]
                    here = pl.ds(r, ROWS)
                    value = (1.0 - OMEGA) * planes[p][t] + sq[p, here, lane(t)]
                    value = value + scale_ref[p, here, lane(t)] * beside
                    if not final:
                        dst[p, pl.ds(r + ROWS, ROWS), lane(t)] = value
                    elif p < span // 2:
                        lo_ref[p, here, lane(t)] = value
                    else:
                        hi_ref[p - span // 2, here, lane(t)] = value
            return carry

        lax.fori_loop(0, rows // ROWS, body, 0, unroll=UNROLL)
        src, dst = dst, src


def solve(order, extra, resid, scale):
    span, rows, depth = scale.shape
    half = jax.ShapeDtypeStruct((span // 2, rows, depth), jnp.float32)
    padded = pltpu.VMEM((span, rows + 2 * ROWS, depth), jnp.float32)
    return pl.pallas_call(
        functools.partial(solve_kernel, order),
        out_shape=(half, half),
        in_specs=[pl.BlockSpec(memory_space=pltpu.VMEM)] * 3,
        out_specs=(pl.BlockSpec(memory_space=pltpu.VMEM),) * 2,
        scratch_shapes=[pltpu.VMEM((span, rows, depth), jnp.float32), padded, padded],
        compiler_params=pltpu.CompilerParams(vmem_limit_bytes=24 << 20),
        cost_estimate=pl.CostEstimate(
            flops=SWEEPS * 40 * span * rows * depth,
            bytes_accessed=20 * span * rows * depth,
            transcendentals=0,
        ),
        name="solve",
    )(extra, resid, scale)


def image_kernel(order, n, part_0, part_1, part_2, diag_ref, resid_ref, prev_ref, image_ref, dots_ref):
    count, rows, depth = diag_ref.shape
    tiles = depth // LANES
    parts = (part_0, part_1, part_2)
    rim = RIM // ROWS
    start = lax.axis_index("colour") * rim
    steps = rows // ROWS

    def body(j, carry):
        upper, lower = carry
        r = pl.multiple_of(j * ROWS, ROWS)
        below = pl.multiple_of(jnp.maximum(j - 1, 0) * ROWS, ROWS)
        above = pl.multiple_of(jnp.minimum(j + 1, steps - 1) * ROWS, ROWS)
        has_below = (j > 0).astype(jnp.float32)
        has_above = (j + 1 < steps).astype(jnp.float32)
        own = ((j >= start) & (j < start + steps - rim)).astype(jnp.float32)
        here = pl.ds(r, ROWS)
        planes = [[parts[k][at, here, lane(t)] for t in range(tiles)] for k, at in order]
        for p in range(count):
            k, at = order[p + 1]
            for t in range(tiles):
                before = parts[k][at, pl.ds(below, ROWS), lane(t)] * has_below
                after = parts[k][at, pl.ds(above, ROWS), lane(t)] * has_above
                beside = lateral(planes, p + 1, t, before, after)
                beside = beside + planes[p][t] + planes[p + 2][t]
                centre = planes[p + 1][t]
                value = (6.0 + diag_ref[p, here, lane(t)]) * centre - beside
                image_ref[p, here, lane(t)] = value
                weighted = centre * own
                upper = upper + resid_ref[p, here, lane(t)] * weighted
                lower = lower + weighted * value
        return upper, lower

    zero = jnp.zeros((ROWS, LANES), jnp.float32)
    upper, lower = lax.fori_loop(0, steps, body, (zero, zero), unroll=2)
    at = lax.broadcasted_iota(jnp.int32, (ROWS, LANES), 0)
    found = jnp.where(at == 2 * n + 1, jnp.sum(lower), prev_ref[...])
    dots_ref[...] = jnp.where(at == 2 * n, jnp.sum(upper), found)


def image_of(order, n, parts, diag, resid, prev):
    count, rows, depth = diag.shape
    return pl.pallas_call(
        functools.partial(image_kernel, order, n),
        out_shape=(
            jax.ShapeDtypeStruct((count, rows, depth), jnp.float32),
            jax.ShapeDtypeStruct((ROWS, LANES), jnp.float32),
        ),
        in_specs=[pl.BlockSpec(memory_space=pltpu.VMEM)] * 6,
        out_specs=(pl.BlockSpec(memory_space=pltpu.VMEM),) * 2,
        compiler_params=pltpu.CompilerParams(vmem_limit_bytes=16 << 20),
        cost_estimate=pl.CostEstimate(
            flops=80 * count * rows * depth,
            bytes_accessed=20 * count * rows * depth,
            transcendentals=0,
        ),
        name="image",
    )(*parts, diag, resid, prev)


def alpha_of(n, dots_ref):
    ratio = dots_ref[2 * n : 2 * n + 1, :] / dots_ref[2 * n + 1 : 2 * n + 2, :]
    return jnp.broadcast_to(ratio, (ROWS, LANES))


def update_kernel(n, dots_ref, resid_ref, image_ref, first_ref, out_ref):
    count, rows, depth = resid_ref.shape
    alpha = alpha_of(n, dots_ref)

    def body(j, carry):
        here = pl.ds(pl.multiple_of(j * ROWS, ROWS), ROWS)
        for p in range(count):
            for t in range(depth // LANES):
                value = resid_ref[p, here, lane(t)] - alpha * image_ref[p, here, lane(t)]
                out_ref[p, here, lane(t)] = value
                if p == 0:
                    first_ref[0, here, lane(t)] = value
        return carry

    lax.fori_loop(0, rows // ROWS, body, 0)


def update(n, dots, resid, image):
    count, rows, depth = resid.shape
    return pl.pallas_call(
        functools.partial(update_kernel, n),
        out_shape=(
            jax.ShapeDtypeStruct((1, rows, depth), jnp.float32),
            jax.ShapeDtypeStruct(resid.shape, jnp.float32),
        ),
        in_specs=[pl.BlockSpec(memory_space=pltpu.VMEM)] * 3,
        out_specs=(pl.BlockSpec(memory_space=pltpu.VMEM),) * 2,
        compiler_params=pltpu.CompilerParams(vmem_limit_bytes=16 << 20),
        cost_estimate=pl.CostEstimate(
            flops=4 * count * rows * depth,
            bytes_accessed=12 * count * rows * depth,
            transcendentals=0,
        ),
        name="update",
    )(dots, resid, image)


def finish_kernel(
    order_0, order_1, n, dots_0, dots_1, a_0, a_1, a_2, b_0, b_1, b_2, resid_ref, image_ref,
    prev_ref, kept_ref, sent_ref, norm_ref,
):
    count, rows, depth = resid_ref.shape
    half = depth // 2
    me = lax.axis_index("colour")
    alpha_0 = alpha_of(n, dots_0)
    alpha_1 = alpha_of(n, dots_1)
    first, second = (a_0, a_1, a_2), (b_0, b_1, b_2)

    def body(j, acc):
        here = pl.ds(pl.multiple_of(me * RIM + j * ROWS, ROWS), ROWS)
        there = pl.ds(pl.multiple_of(j * ROWS, ROWS), ROWS)
        for out, side in ((kept_ref, me), (sent_ref, 1 - me)):
            for t in range(half // LANES):
                at_z = pl.ds(pl.multiple_of(side * half + t * LANES, LANES), LANES)
                for p in range(count):
                    k, at = order_0[p + 1]
                    m, to = order_1[p + 1]
                    u = alpha_0 * first[k][at, here, at_z] + alpha_1 * second[m][to, here, at_z]
                    q = resid_ref[p, here, at_z] - alpha_1 * image_ref[p, here, at_z]
                    out[0, p, there, lane(t)] = u
                    out[1, p, there, lane(t)] = q
                    acc = acc + q * q
        return acc

    steps = kept_ref.shape[2] // ROWS
    acc = lax.fori_loop(0, steps, body, jnp.zeros((ROWS, LANES), jnp.float32))
    at = lax.broadcasted_iota(jnp.int32, (ROWS, LANES), 0)
    norm_ref[...] = jnp.where(at == n, jnp.sum(acc), prev_ref[...])


def finish(order_0, order_1, n, dots_0, dots_1, parts_0, parts_1, resid, image, prev):
    count, rows, depth = resid.shape
    block = jax.ShapeDtypeStruct((2, count, rows - RIM, depth // 2), jnp.float32)
    return pl.pallas_call(
        functools.partial(finish_kernel, order_0, order_1, n),
        out_shape=(block, block, jax.ShapeDtypeStruct((ROWS, LANES), jnp.float32)),
        in_specs=[pl.BlockSpec(memory_space=pltpu.VMEM)] * 11,
        out_specs=(pl.BlockSpec(memory_space=pltpu.VMEM),) * 3,
        compiler_params=pltpu.CompilerParams(vmem_limit_bytes=24 << 20),
        cost_estimate=pl.CostEstimate(
            flops=8 * count * rows * depth,
            bytes_accessed=24 * count * rows * depth,
            transcendentals=0,
        ),
        name="finish",
    )(dots_0, dots_1, *parts_0, *parts_1, resid, image, prev)


def total_kernel(count, mine_ref, out_ref, slots, local_sem, send_sem, recv_sem):
    sub = lax.axis_index("sub")
    colour = lax.axis_index("colour")
    me = sub + colour * count
    levels = count.bit_length() - 1
    partners = []
    for level in range(levels):
        bit = (sub // 2**level) % 2
        partners.append((colour, sub + (1 - 2 * bit) * 2**level))
    partners.append((1 - colour, sub))
    barrier = pltpu.get_barrier_semaphore()
    for partner in partners:
        pl.semaphore_signal(
            barrier, inc=1, device_id=partner, device_id_type=pl.DeviceIdType.MESH
        )
    own = pltpu.make_async_copy(mine_ref, slots.at[me], local_sem)
    own.start()
    pl.semaphore_wait(barrier, len(partners))
    own.wait()
    for level, partner in enumerate(partners):
        size = 2**level
        block = slots.at[pl.ds((me // size) * size, size)]
        copy = pltpu.make_async_remote_copy(
            src_ref=block,
            dst_ref=block,
            send_sem=send_sem.at[level],
            recv_sem=recv_sem.at[level],
            device_id=partner,
            device_id_type=pl.DeviceIdType.MESH,
        )
        copy.start()
        copy.wait()
    out_ref[...] = jnp.sum(slots[...], axis=0)


def total_of(count, mine, key):
    levels = count.bit_length()
    assert count == 2 ** (levels - 1)
    return pl.pallas_call(
        functools.partial(total_kernel, count),
        out_shape=jax.ShapeDtypeStruct(mine.shape, jnp.float32),
        in_specs=[pl.BlockSpec(memory_space=pltpu.VMEM)],
        out_specs=pl.BlockSpec(memory_space=pltpu.VMEM),
        scratch_shapes=[
            pltpu.VMEM((2 * count,) + mine.shape, jnp.float32),
            pltpu.SemaphoreType.DMA,
            pltpu.SemaphoreType.DMA((levels,)),
            pltpu.SemaphoreType.DMA((levels,)),
        ],
        compiler_params=pltpu.CompilerParams(collective_id=key, has_side_effects=True),
        cost_estimate=pl.CostEstimate(flops=20000000, bytes_accessed=20000000, transcendentals=0),
        name="total",
    )(mine)


ORDER_0 = ((0, 0), (0, 1), (1, 0), (1, 1), (2, 0), (2, 1))
ORDER_1 = ((2, 0), (2, 1), (0, 0), (0, 1), (1, 0), (1, 1))


def shards(rhs, diagonal):
    colour = lax.axis_index("colour")
    device = lax.axis_index("sub")
    count = lax.axis_size("sub")
    nrhs, _, ny, _ = rhs.shape
    rows = ny // 2 + RIM
    begin = colour * (ny // 2 - RIM)
    to_right = [(i, i + 1) for i in range(count - 1)]
    to_left = [(i + 1, i) for i in range(count - 1)]

    source = lax.dynamic_slice_in_dim(rhs, begin, rows, 2)
    diag = lax.dynamic_slice_in_dim(diagonal, begin, rows, 1)
    diag_low = lax.ppermute(diag[-1:], "sub", to_right)
    low = [lax.ppermute(source[n, -1:], "sub", to_right) for n in range(nrhs)]
    diag_high = lax.ppermute(diag[:1], "sub", to_left)
    has_low = (device > 0).astype(jnp.float32)
    has_high = (device < count - 1).astype(jnp.float32)
    scale = OMEGA / (6.0 + diag)
    scale_0 = jnp.concatenate([has_low * (OMEGA / (6.0 + diag_low)), scale[:-1]], axis=0)
    scale_1 = jnp.concatenate([scale[1:], has_high * (OMEGA / (6.0 + diag_high))], axis=0)

    q = [source[n] for n in range(nrhs)]
    parts_0, parts_1 = [], []
    blank = jnp.zeros((ROWS, LANES), jnp.float32)
    images, q1, high = [], [], []
    for n in range(nrhs):
        lo, hi = solve((-1, 0, 1, 2), low[n], q[n], scale_0)
        parts_0.append((lo, hi, lax.ppermute(lo, "sub", to_left)))
    dots = blank
    for n in range(nrhs):
        image, dots = image_of(ORDER_0, n, parts_0[n], diag, q[n], dots)
        images.append(image)
    dots_0 = total_of(count, dots, 0)
    for n in range(nrhs):
        edge, resid = update(n, dots_0, q[n], images[n])
        q1.append(resid)
        high.append(lax.ppermute(edge, "sub", to_left))
    for n in range(nrhs):
        lo, hi = solve((1, 2, 3, -1), high[n], q1[n], scale_1)
        parts_1.append((lo, hi, lax.ppermute(hi, "sub", to_right)))
    images = []
    dots = blank
    for n in range(nrhs):
        image, dots = image_of(ORDER_1, n, parts_1[n], diag, q1[n], dots)
        images.append(image)
    dots_1 = total_of(count, dots, 1)
    solved, left = [], []
    norm = blank
    first = colour == 0
    for n in range(nrhs):
        kept, sent, norm = finish(
            ORDER_0, ORDER_1, n, dots_0, dots_1, parts_0[n], parts_1[n], q1[n], images[n], norm
        )
        got = lax.ppermute(sent, "colour", [(0, 1), (1, 0)])
        whole = jnp.concatenate([jnp.where(first, kept, got), jnp.where(first, got, kept)], axis=2)
        solved.append(whole[0])
        left.append(whole[1])
    squares = total_of(count, norm, 2)[:nrhs, 0]
    return jnp.stack(solved), jnp.stack(left), jnp.sqrt(squares)


def solution(mesh):
    placed = (P(None, "sub", None, None), P("sub", None, None))
    return jax.shard_map(
        shards,
        mesh=mesh,
        in_specs=placed,
        out_specs=(P(None, "sub", None, "colour"), P(None, "sub", None, "colour"), P()),
        check_vma=False,
    )
```

profile of v0, /device:TPU:0, one launch (start us, length us, event | category | flops | bytes accessed | tf_op | source)
XLA Modules:
  0.0 240.7 jit_solution(567201850066462212)
XLA Ops:
  0.6 1.9 constant_dynamic-slice_fusion.1
  2.6 5.6 %collective-permute-start.1 = (f32[1,144,512]{2,1,0:T(8,128)}, f32[1,144,512]{2,1,0:T(8,128)}, u32[]{:S(2)}, u32[]{:S(2)}) collective-permute-start(f32[1,144,512]{2,1,0:T(8,128)} %get-tuple-element.96), channel_id=1, source_target_pairs={{0,1},{1,2},{2,3},{3,4},{4,5},{5,6},{6,7},{7,8},{8,9},{9,10},{10,1... | collective-permute-start | bytes 884744 | tf_op jit(solution)/shard_map/ppermute | solution.py:339
  8.2 2.1 dynamic-slice_bitcast_fusion.3
  10.3 3.4 %collective-permute-start.5 = (f32[1,144,512]{2,1,0:T(8,128)}, f32[1,144,512]{2,1,0:T(8,128)}, u32[]{:S(2)}, u32[]{:S(2)}) collective-permute-start(f32[1,144,512]{2,1,0:T(8,128)} %get-tuple-element.86), channel_id=1, source_target_pairs={{0,1},{1,2},{2,3},{3,4},{4,5},{5,6},{6,7},{7,8},{8,9},{9,10},{10,1... | collective-permute-start | bytes 884744 | tf_op jit(solution)/shard_map/ppermute | solution.py:340
  13.7 3.4 %collective-permute-start.3 = (f32[1,144,512]{2,1,0:T(8,128)}, f32[1,144,512]{2,1,0:T(8,128)}, u32[]{:S(2)}, u32[]{:S(2)}) collective-permute-start(f32[1,144,512]{2,1,0:T(8,128)} %get-tuple-element.87), channel_id=1, source_target_pairs={{0,1},{1,2},{2,3},{3,4},{4,5},{5,6},{6,7},{7,8},{8,9},{9,10},{10,1... | collective-permute-start | bytes 884744 | tf_op jit(solution)/shard_map/ppermute | solution.py:340
  17.1 3.5 %collective-permute-start = (f32[1,144,512]{2,1,0:T(8,128)}, f32[1,144,512]{2,1,0:T(8,128)}, u32[]{:S(2)}, u32[]{:S(2)}) collective-permute-start(f32[1,144,512]{2,1,0:T(8,128)} %get-tuple-element.88), channel_id=1, source_target_pairs={{0,1},{1,2},{2,3},{3,4},{4,5},{5,6},{6,7},{7,8},{8,9},{9,10},{10,1... | collective-permute-start | bytes 884744 | tf_op jit(solution)/shard_map/ppermute | solution.py:340
  20.6 3.6 %dynamic-slice_bitcast_fusion = (f32[4,144,512]{2,1,0:T(8,128)}, f32[4,144,512]{2,1,0:T(8,128)S(1)}, f32[4,144,512]{2,1,0:T(8,128)S(1)}) fusion(f32[3,4,256,512]{3,2,1,0:T(8,128)} %param.2, s32[]{:T(128)S(6)} %select_n.33, s32[]{:T(128)S(6)} %add.26, s32[]{:T(128)S(6)} %add.22), kind=kLoop, calls=%fused_computation.16 | loop fusion | bytes 7077900 | tf_op jit(solution)/shard_map/squeeze | solution.py:348
  25.5 2.6 %fusion.6 = (f32[3,144,512]{2,1,0:T(8,128)}, f32[3,144,512]{2,1,0:T(8,128)S(1)}) fusion(f32[4,144,512]{2,1,0:T(8,128)} %get-tuple-element.81), kind=kLoop, calls=%fused_computation.40 | loop fusion | bytes 3538944 | tf_op jit(solution)/shard_map/slice | solution.py:346
  29.4 7.8 %solve.8 = (f32[2,144,512]{2,1,0:T(8,128)}, f32[2,144,512]{2,1,0:T(8,128)S(1)}) custom-call(f32[1,144,512]{2,1,0:T(8,128)} %collective-permute-done.5.extra_ref, f32[4,144,512]{2,1,0:T(8,128)S(1)} %copy-done, f32[4,144,512]{2,1,0:T(8,128)S(1)} %pad_maximum_fusion.2.scale_ref), custom_call_target="tpu_custom_call" | custom-call | flops 94371840 | bytes 5898240 | tf_op jit(solution)/shard_map/solve/pallas_call | solution.py:99
  38.1 1.3 collective-permute-start.6
  39.4 7.8 %solve.7 = (f32[2,144,512]{2,1,0:T(8,128)}, f32[2,144,512]{2,1,0:T(8,128)S(1)}) custom-call(f32[1,144,512]{2,1,0:T(8,128)} %collective-permute-done.3.extra_ref, f32[4,144,512]{2,1,0:T(8,128)S(1)} %get-tuple-element.84.resid_ref, f32[4,144,512]{2,1,0:T(8,128)S(1)} %pad_maximum_fusion.2.scale_ref), custom_call_target="tpu_custom_call" | custom-call | flops 94371840 | bytes 5898240 | tf_op jit(solution)/shard_map/solve/pallas_call | solution.py:99
  48.0 1.3 collective-permute-start.4
  49.3 7.8 %solve.6 = (f32[2,144,512]{2,1,0:T(8,128)}, f32[2,144,512]{2,1,0:T(8,128)S(1)}) custom-call(f32[1,144,512]{2,1,0:T(8,128)} %collective-permute-done.extra_ref, f32[4,144,512]{2,1,0:T(8,128)S(1)} %get-tuple-element.85.resid_ref, f32[4,144,512]{2,1,0:T(8,128)S(1)} %pad_maximum_fusion.2.scale_ref), custom_call_target="tpu_custom_call" | custom-call | flops 94371840 | bytes 5898240 | tf_op jit(solution)/shard_map/solve/pallas_call | solution.py:99
  57.9 1.3 collective-permute-start.2
  59.2 1.3 collective-permute-start.8
  62.9 2.7 %image.6 = (f32[4,144,512]{2,1,0:T(8,128)S(1)}, f32[8,128]{1,0:T(8,128)S(1)}) custom-call(f32[2,144,512]{2,1,0:T(8,128)} %get-tuple-element.46.part_0.a_0, f32[2,144,512]{2,1,0:T(8,128)S(1)} %copy-done.14, f32[2,144,512]{2,1,0:T(8,128)} %collective-permute-done.6.part_2.a_2, f32[4,144,512]{2,1,0:T(8,128)S(1)} %get-tuple-element.82.diag_ref, ...), custom_call_target="tpu_custom_call" | custom-call | flops 23592960 | bytes 5898240 | tf_op jit(solution)/shard_map/image/pallas_call | solution.py:157
  65.6 3.3 %collective-permute-done.4.part_2.a_2 = f32[2,144,512]{2,1,0:T(8,128)} collective-permute-done((f32[2,144,512]{2,1,0:T(8,128)}, f32[2,144,512]{2,1,0:T(8,128)}, u32[]{:S(2)}, u32[]{:S(2)}) %collective-permute-start.4) | collective-permute-done | bytes 589856 | tf_op jit(solution)/shard_map/ppermute | solution.py:354
  68.9 2.7 %image.7 = (f32[4,144,512]{2,1,0:T(8,128)S(1)}, f32[8,128]{1,0:T(8,128)S(1)}) custom-call(f32[2,144,512]{2,1,0:T(8,128)} %get-tuple-element.44.part_0.a_0, f32[2,144,512]{2,1,0:T(8,128)S(1)} %copy-done.11, f32[2,144,512]{2,1,0:T(8,128)} %collective-permute-done.4.part_2.a_2, f32[4,144,512]{2,1,0:T(8,128)S(1)} %get-tuple-element.82.diag_ref, ...), custom_call_target="tpu_custom_call" | custom-call | flops 23592960 | bytes 5898240 | tf_op jit(solution)/shard_map/image/pallas_call | solution.py:157
  71.6 10.0 %collective-permute-done.2.part_2.a_2 = f32[2,144,512]{2,1,0:T(8,128)} collective-permute-done((f32[2,144,512]{2,1,0:T(8,128)}, f32[2,144,512]{2,1,0:T(8,128)}, u32[]{:S(2)}, u32[]{:S(2)}) %collective-permute-start.2) | collective-permute-done | bytes 589856 | tf_op jit(solution)/shard_map/ppermute | solution.py:354
  81.6 2.7 %image.8 = (f32[4,144,512]{2,1,0:T(8,128)S(1)}, f32[8,128]{1,0:T(8,128)S(1)}) custom-call(f32[2,144,512]{2,1,0:T(8,128)} %get-tuple-element.42.part_0.a_0, f32[2,144,512]{2,1,0:T(8,128)S(1)} %copy-done.8, f32[2,144,512]{2,1,0:T(8,128)} %collective-permute-done.2.part_2.a_2, f32[4,144,512]{2,1,0:T(8,128)S(1)} %get-tuple-element.82.diag_ref, ...), custom_call_target="tpu_custom_call" | custom-call | flops 23592960 | bytes 5898240 | tf_op jit(solution)/shard_map/image/pallas_call | solution.py:157
  85.8 17.7 %total.3.dots_ref.dots_0 = f32[8,128]{1,0:T(8,128)} custom-call(f32[8,128]{1,0:T(8,128)} %copy-done.57), custom_call_target="tpu_custom_call" | custom-call | flops 20000000 | bytes 20000000 | tf_op jit(solution)/shard_map/total/pallas_call | solution.py:306
  104.9 1.3 copy-done.45
  107.1 1.6 collective-permute-start.12
  108.9 1.4 collective-permute-start.10
  110.6 1.3 collective-permute-start.7
  113.0 12.4 %collective-permute-done.10.extra_ref = f32[1,144,512]{2,1,0:T(8,128)S(1)} collective-permute-done((f32[1,144,512]{2,1,0:T(8,128)S(1)}, f32[1,144,512]{2,1,0:T(8,128)S(1)}, u32[]{:S(2)}, u32[]{:S(2)}) %collective-permute-start.10) | collective-permute-done | bytes 294944 | tf_op jit(solution)/shard_map/ppermute | solution.py:363
  125.4 6.0 %solve.10 = (f32[2,144,512]{2,1,0:T(8,128)S(1)}, f32[2,144,512]{2,1,0:T(8,128)S(1)}) custom-call(f32[1,144,512]{2,1,0:T(8,128)S(1)} %collective-permute-done.10.extra_ref, f32[4,144,512]{2,1,0:T(8,128)S(1)} %get-tuple-element.58.resid_ref, f32[4,144,512]{2,1,0:T(8,128)S(1)} %pad_maximum_fusion.3.scale_ref), custom_call_target="tpu_custom_call" | custom-call | flops 94371840 | bytes 5898240 | tf_op jit(solution)/shard_map/solve/pallas_call | solution.py:99
  131.5 2.6 %collective-permute-start.11 = (f32[2,144,512]{2,1,0:T(8,128)S(1)}, f32[2,144,512]{2,1,0:T(8,128)S(1)}, u32[]{:S(2)}, u32[]{:S(2)}) collective-permute-start(f32[2,144,512]{2,1,0:T(8,128)S(1)} %get-tuple-element.60.part_1.b_1), channel_id=1, source_target_pairs={{0,1},{1,2},{2,3},{3,4},{4,5},{5,6},{6,7},{7,8},{8,9},{9,10},{10,1... | collective-permute-start | bytes 1769480 | tf_op jit(solution)/shard_map/ppermute | solution.py:366
  134.1 6.0 %solve.11 = (f32[2,144,512]{2,1,0:T(8,128)S(1)}, f32[2,144,512]{2,1,0:T(8,128)S(1)}) custom-call(f32[1,144,512]{2,1,0:T(8,128)S(1)} %collective-permute-done.12.extra_ref, f32[4,144,512]{2,1,0:T(8,128)S(1)} %get-tuple-element.63.resid_ref, f32[4,144,512]{2,1,0:T(8,128)S(1)} %pad_maximum_fusion.3.scale_ref), custom_call_target="tpu_custom_call" | custom-call | flops 94371840 | bytes 5898240 | tf_op jit(solution)/shard_map/solve/pallas_call | solution.py:99
  140.2 2.5 %collective-permute-start.13 = (f32[2,144,512]{2,1,0:T(8,128)S(1)}, f32[2,144,512]{2,1,0:T(8,128)S(1)}, u32[]{:S(2)}, u32[]{:S(2)}) collective-permute-start(f32[2,144,512]{2,1,0:T(8,128)S(1)} %get-tuple-element.65.part_1.b_1), channel_id=1, source_target_pairs={{0,1},{1,2},{2,3},{3,4},{4,5},{5,6},{6,7},{7,8},{8,9},{9,10},{10,1... | collective-permute-start | bytes 1769480 | tf_op jit(solution)/shard_map/ppermute | solution.py:366
  142.7 6.0 %solve.9 = (f32[2,144,512]{2,1,0:T(8,128)S(1)}, f32[2,144,512]{2,1,0:T(8,128)S(1)}) custom-call(f32[1,144,512]{2,1,0:T(8,128)S(1)} %collective-permute-done.7.extra_ref, f32[4,144,512]{2,1,0:T(8,128)S(1)} %get-tuple-element.53.resid_ref, f32[4,144,512]{2,1,0:T(8,128)S(1)} %pad_maximum_fusion.3.scale_ref), custom_call_target="tpu_custom_call" | custom-call | flops 94371840 | bytes 5898240 | tf_op jit(solution)/shard_map/solve/pallas_call | solution.py:99
  148.7 4.2 %collective-permute-start.9 = (f32[2,144,512]{2,1,0:T(8,128)S(1)}, f32[2,144,512]{2,1,0:T(8,128)S(1)}, u32[]{:S(2)}, u32[]{:S(2)}) collective-permute-start(f32[2,144,512]{2,1,0:T(8,128)S(1)} %get-tuple-element.55.part_1.b_1), channel_id=1, source_target_pairs={{0,1},{1,2},{2,3},{3,4},{4,5},{5,6},{6,7},{7,8},{8,9},{9,10},{10,1... | collective-permute-start | bytes 1769480 | tf_op jit(solution)/shard_map/ppermute | solution.py:366
  153.0 7.3 %collective-permute-done.13.part_2.b_2 = f32[2,144,512]{2,1,0:T(8,128)S(1)} collective-permute-done((f32[2,144,512]{2,1,0:T(8,128)S(1)}, f32[2,144,512]{2,1,0:T(8,128)S(1)}, u32[]{:S(2)}, u32[]{:S(2)}) %collective-permute-start.13) | collective-permute-done | bytes 589856 | tf_op jit(solution)/shard_map/ppermute | solution.py:366
  160.3 1.4 image.9
  161.8 1.4 image.10
  164.2 6.6 %collective-permute-done.9.part_2.b_2 = f32[2,144,512]{2,1,0:T(8,128)S(1)} collective-permute-done((f32[2,144,512]{2,1,0:T(8,128)S(1)}, f32[2,144,512]{2,1,0:T(8,128)S(1)}, u32[]{:S(2)}, u32[]{:S(2)}) %collective-permute-start.9) | collective-permute-done | bytes 589856 | tf_op jit(solution)/shard_map/ppermute | solution.py:366
  170.8 1.4 image.11
  173.9 17.8 %total.4.dots_1 = f32[8,128]{1,0:T(8,128)} custom-call(f32[8,128]{1,0:T(8,128)} %copy-done.56), custom_call_target="tpu_custom_call" | custom-call | flops 20000000 | bytes 20000000 | tf_op jit(solution)/shard_map/total/pallas_call | solution.py:306
  195.9 1.3 copy-done.39
  197.9 3.1 %finish.3 = (f32[2,4,128,256]{3,2,1,0:T(8,128)S(1)}, f32[2,4,128,256]{3,2,1,0:T(8,128)}, f32[8,128]{1,0:T(8,128)S(1)}) custom-call(f32[8,128]{1,0:T(8,128)S(1)} %copy-done.52, f32[8,128]{1,0:T(8,128)S(1)} %copy-done.53, f32[2,144,512]{2,1,0:T(8,128)} %get-tuple-element.46.part_0.a_0, f32[2,144,512]{2,1,0:T(8,128)S(1)} %copy-done.15, ...), custom_call_target="tpu_custom_call" | custom-call | flops 2359296 | bytes 7077888 | tf_op jit(solution)/shard_map/finish/pallas_call | solution.py:253
  202.1 3.0 %finish.4 = (f32[2,4,128,256]{3,2,1,0:T(8,128)S(1)}, f32[2,4,128,256]{3,2,1,0:T(8,128)}, f32[8,128]{1,0:T(8,128)S(1)}) custom-call(f32[8,128]{1,0:T(8,128)S(1)} %copy-done.52, f32[8,128]{1,0:T(8,128)S(1)} %copy-done.54, f32[2,144,512]{2,1,0:T(8,128)} %get-tuple-element.44.part_0.a_0, f32[2,144,512]{2,1,0:T(8,128)S(1)} %copy-done.12, ...), custom_call_target="tpu_custom_call" | custom-call | flops 2359296 | bytes 7077888 | tf_op jit(solution)/shard_map/finish/pallas_call | solution.py:253
  208.8 2.9 %finish.5 = (f32[2,4,128,256]{3,2,1,0:T(8,128)S(1)}, f32[2,4,128,256]{3,2,1,0:T(8,128)}, f32[8,128]{1,0:T(8,128)S(1)}) custom-call(f32[8,128]{1,0:T(8,128)S(1)} %copy-done.52, f32[8,128]{1,0:T(8,128)S(1)} %copy-done.54, f32[2,144,512]{2,1,0:T(8,128)} %get-tuple-element.42.part_0.a_0, f32[2,144,512]{2,1,0:T(8,128)S(1)} %copy-done.9, ...), custom_call_target="tpu_custom_call" | custom-call | flops 2359296 | bytes 7077888 | tf_op jit(solution)/shard_map/finish/pallas_call | solution.py:253
  213.4 16.2 %total.5 = f32[8,128]{1,0:T(8,128)} custom-call(f32[8,128]{1,0:T(8,128)} %copy-done.55), custom_call_target="tpu_custom_call" | custom-call | flops 20000000 | bytes 20000000 | tf_op jit(solution)/shard_map/total/pallas_call | solution.py:306
  229.6 1.3 sqrt_reduce_fusion
  230.9 1.8 broadcast_select_fusion.4
  233.9 1.4 broadcast_select_fusion.2
  236.7 1.9 fusion
  238.7 2.1 pad_maximum_fusion.1
  (146 shorter events, 29.5 us)
Async XLA Ops:
  2.6 25.5 %collective-permute-start.1 = (f32[1,144,512]{2,1,0:T(8,128)}, f32[1,144,512]{2,1,0:T(8,128)}, u32[]{:S(2)}, u32[]{:S(2)}) collective-permute-start(f32[1,144,512]{2,1,0:T(8,128)} %get-tuple-element.96), channel_id=1, source_target_pairs={{0,1},{1,2},{2,3},{3,4},{4,5},{5,6},{6,7},{7,8},{8,9},{9,10},{10,1... | collective-permute-start | bytes 884744 | tf_op jit(solution)/shard_map/ppermute | solution.py:339
  10.3 19.0 %collective-permute-start.5 = (f32[1,144,512]{2,1,0:T(8,128)}, f32[1,144,512]{2,1,0:T(8,128)}, u32[]{:S(2)}, u32[]{:S(2)}) collective-permute-start(f32[1,144,512]{2,1,0:T(8,128)} %get-tuple-element.86), channel_id=1, source_target_pairs={{0,1},{1,2},{2,3},{3,4},{4,5},{5,6},{6,7},{7,8},{8,9},{9,10},{10,1... | collective-permute-start | bytes 884744 | tf_op jit(solution)/shard_map/ppermute | solution.py:340
  13.7 25.7 %collective-permute-start.3 = (f32[1,144,512]{2,1,0:T(8,128)}, f32[1,144,512]{2,1,0:T(8,128)}, u32[]{:S(2)}, u32[]{:S(2)}) collective-permute-start(f32[1,144,512]{2,1,0:T(8,128)} %get-tuple-element.87), channel_id=1, source_target_pairs={{0,1},{1,2},{2,3},{3,4},{4,5},{5,6},{6,7},{7,8},{8,9},{9,10},{10,1... | collective-permute-start | bytes 884744 | tf_op jit(solution)/shard_map/ppermute | solution.py:340
  17.1 7.1 %copy-start.59 = (f32[4,256,512]{2,1,0:T(8,128)S(1)}, f32[4,256,512]{2,1,0:T(8,128)}, u32[]{:S(2)}) copy-start(f32[4,256,512]{2,1,0:T(8,128)} %param.3) | copy-start | bytes 6291460
  17.1 32.2 %collective-permute-start = (f32[1,144,512]{2,1,0:T(8,128)}, f32[1,144,512]{2,1,0:T(8,128)}, u32[]{:S(2)}, u32[]{:S(2)}) collective-permute-start(f32[1,144,512]{2,1,0:T(8,128)} %get-tuple-element.88), channel_id=1, source_target_pairs={{0,1},{1,2},{2,3},{3,4},{4,5},{5,6},{6,7},{7,8},{8,9},{9,10},{10,1... | collective-permute-start | bytes 884744 | tf_op jit(solution)/shard_map/ppermute | solution.py:340
  38.1 22.4 %collective-permute-start.6 = (f32[2,144,512]{2,1,0:T(8,128)}, f32[2,144,512]{2,1,0:T(8,128)}, u32[]{:S(2)}, u32[]{:S(2)}) collective-permute-start(f32[2,144,512]{2,1,0:T(8,128)} %get-tuple-element.46.part_0.a_0), channel_id=1, source_target_pairs={{1,0},{2,1},{3,2},{4,3},{5,4},{6,5},{7,6},{8,7},{9,8},{10,9},{11,1... | collective-permute-start | bytes 1769480 | tf_op jit(solution)/shard_map/ppermute | solution.py:354
  48.0 20.9 %collective-permute-start.4 = (f32[2,144,512]{2,1,0:T(8,128)}, f32[2,144,512]{2,1,0:T(8,128)}, u32[]{:S(2)}, u32[]{:S(2)}) collective-permute-start(f32[2,144,512]{2,1,0:T(8,128)} %get-tuple-element.44.part_0.a_0), channel_id=1, source_target_pairs={{1,0},{2,1},{3,2},{4,3},{5,4},{6,5},{7,6},{8,7},{9,8},{10,9},{11,1... | collective-permute-start | bytes 1769480 | tf_op jit(solution)/shard_map/ppermute | solution.py:354
  57.9 23.6 %collective-permute-start.2 = (f32[2,144,512]{2,1,0:T(8,128)}, f32[2,144,512]{2,1,0:T(8,128)}, u32[]{:S(2)}, u32[]{:S(2)}) collective-permute-start(f32[2,144,512]{2,1,0:T(8,128)} %get-tuple-element.42.part_0.a_0), channel_id=1, source_target_pairs={{1,0},{2,1},{3,2},{4,3},{5,4},{6,5},{7,6},{8,7},{9,8},{10,9},{11,1... | collective-permute-start | bytes 1769480 | tf_op jit(solution)/shard_map/ppermute | solution.py:354
  59.2 52.7 %collective-permute-start.8 = (f32[1,144,512]{2,1,0:T(8,128)}, f32[1,144,512]{2,1,0:T(8,128)}, u32[]{:S(2)}, u32[]{:S(2)}) collective-permute-start(f32[1,144,512]{2,1,0:T(8,128)} %get-tuple-element.95), channel_id=1, source_target_pairs={{1,0},{2,1},{3,2},{4,3},{5,4},{6,5},{7,6},{8,7},{9,8},{10,9},{11,1... | collective-permute-start | bytes 884744 | tf_op jit(solution)/shard_map/ppermute | solution.py:341
  62.9 6.0 %copy-start.11 = (f32[2,144,512]{2,1,0:T(8,128)S(1)}, f32[2,144,512]{2,1,0:T(8,128)}, u32[]{:S(2)}) copy-start(f32[2,144,512]{2,1,0:T(8,128)} %copy-done.10) | copy-start | bytes 1769476
  65.6 16.0 %copy-start.44 = (f32[4,144,512]{2,1,0:T(8,128)}, f32[4,144,512]{2,1,0:T(8,128)S(1)}, u32[]{:S(2)}) copy-start(f32[4,144,512]{2,1,0:T(8,128)S(1)} %get-tuple-element.61.image_ref) | copy-start | bytes 3538948
  65.6 16.0 %copy-start.8 = (f32[2,144,512]{2,1,0:T(8,128)S(1)}, f32[2,144,512]{2,1,0:T(8,128)}, u32[]{:S(2)}) copy-start(f32[2,144,512]{2,1,0:T(8,128)} %copy-done.7) | copy-start | bytes 1769476
  71.6 12.6 %copy-start.42 = (f32[4,144,512]{2,1,0:T(8,128)}, f32[4,144,512]{2,1,0:T(8,128)S(1)}, u32[]{:S(2)}) copy-start(f32[4,144,512]{2,1,0:T(8,128)S(1)} %get-tuple-element.56.image_ref) | copy-start | bytes 3538948
  106.8 1.8 copy-start.43
  106.8 3.5 %copy-start.41 = (f32[4,144,512]{2,1,0:T(8,128)S(1)}, f32[4,144,512]{2,1,0:T(8,128)}, u32[]{:S(2)}) copy-start(f32[4,144,512]{2,1,0:T(8,128)} %copy-done.40) | copy-start | bytes 3538948
  107.1 53.2 %copy-start.5 = (f32[4,144,512]{2,1,0:T(8,128)}, f32[4,144,512]{2,1,0:T(8,128)S(1)}, u32[]{:S(2)}) copy-start(f32[4,144,512]{2,1,0:T(8,128)S(1)} %get-tuple-element.63.resid_ref) | copy-start | bytes 3538948
  107.1 27.1 %collective-permute-start.12 = (f32[1,144,512]{2,1,0:T(8,128)S(1)}, f32[1,144,512]{2,1,0:T(8,128)S(1)}, u32[]{:S(2)}, u32[]{:S(2)}) collective-permute-start(f32[1,144,512]{2,1,0:T(8,128)S(1)} %get-tuple-element.62), channel_id=1, source_target_pairs={{1,0},{2,1},{3,2},{4,3},{5,4},{6,5},{7,6},{8,7},{9,8},{10,9},{11,1... | collective-permute-start | bytes 884744 | tf_op jit(solution)/shard_map/ppermute | solution.py:363
  108.6 4.3 %copy-start.58 = (f32[3,144,512]{2,1,0:T(8,128)S(1)}, f32[3,144,512]{2,1,0:T(8,128)}, u32[]{:S(2)}) copy-start(f32[3,144,512]{2,1,0:T(8,128)} %get-tuple-element.97) | copy-start | bytes 2654212
  108.9 52.8 %copy-start.3 = (f32[4,144,512]{2,1,0:T(8,128)}, f32[4,144,512]{2,1,0:T(8,128)S(1)}, u32[]{:S(2)}) copy-start(f32[4,144,512]{2,1,0:T(8,128)S(1)} %get-tuple-element.58.resid_ref) | copy-start | bytes 3538948
  108.9 16.5 %collective-permute-start.10 = (f32[1,144,512]{2,1,0:T(8,128)S(1)}, f32[1,144,512]{2,1,0:T(8,128)S(1)}, u32[]{:S(2)}, u32[]{:S(2)}) collective-permute-start(f32[1,144,512]{2,1,0:T(8,128)S(1)} %get-tuple-element.57), channel_id=1, source_target_pairs={{1,0},{2,1},{3,2},{4,3},{5,4},{6,5},{7,6},{8,7},{9,8},{10,9},{11,1... | collective-permute-start | bytes 884744 | tf_op jit(solution)/shard_map/ppermute | solution.py:363
  110.6 32.1 %collective-permute-start.7 = (f32[1,144,512]{2,1,0:T(8,128)S(1)}, f32[1,144,512]{2,1,0:T(8,128)S(1)}, u32[]{:S(2)}, u32[]{:S(2)}) collective-permute-start(f32[1,144,512]{2,1,0:T(8,128)S(1)} %get-tuple-element.52), channel_id=1, source_target_pairs={{1,0},{2,1},{3,2},{4,3},{5,4},{6,5},{7,6},{8,7},{9,8},{10,9},{11,1... | collective-permute-start | bytes 884744 | tf_op jit(solution)/shard_map/ppermute | solution.py:363
  131.5 30.3 %copy-start.16 = (f32[2,144,512]{2,1,0:T(8,128)}, f32[2,144,512]{2,1,0:T(8,128)S(1)}, u32[]{:S(2)}) copy-start(f32[2,144,512]{2,1,0:T(8,128)S(1)} %get-tuple-element.59.part_0.b_0) | copy-start | bytes 1769476
  131.5 30.3 %copy-start.18 = (f32[2,144,512]{2,1,0:T(8,128)}, f32[2,144,512]{2,1,0:T(8,128)S(1)}, u32[]{:S(2)}) copy-start(f32[2,144,512]{2,1,0:T(8,128)S(1)} %get-tuple-element.60.part_1.b_1) | copy-start | bytes 1769476
  131.5 30.2 %collective-permute-start.11 = (f32[2,144,512]{2,1,0:T(8,128)S(1)}, f32[2,144,512]{2,1,0:T(8,128)S(1)}, u32[]{:S(2)}, u32[]{:S(2)}) collective-permute-start(f32[2,144,512]{2,1,0:T(8,128)S(1)} %get-tuple-element.60.part_1.b_1), channel_id=1, source_target_pairs={{0,1},{1,2},{2,3},{3,4},{4,5},{5,6},{6,7},{7,8},{8,9},{9,10},{10,1... | collective-permute-start | bytes 1769480 | tf_op jit(solution)/shard_map/ppermute | solution.py:366
  140.2 21.5 %copy-start.28 = (f32[2,144,512]{2,1,0:T(8,128)}, f32[2,144,512]{2,1,0:T(8,128)S(1)}, u32[]{:S(2)}) copy-start(f32[2,144,512]{2,1,0:T(8,128)S(1)} %get-tuple-element.64.part_0.b_0) | copy-start | bytes 1769476
  140.2 21.5 %copy-start.30 = (f32[2,144,512]{2,1,0:T(8,128)}, f32[2,144,512]{2,1,0:T(8,128)S(1)}, u32[]{:S(2)}) copy-start(f32[2,144,512]{2,1,0:T(8,128)S(1)} %get-tuple-element.65.part_1.b_1) | copy-start | bytes 1769476
  140.2 20.1 %collective-permute-start.13 = (f32[2,144,512]{2,1,0:T(8,128)S(1)}, f32[2,144,512]{2,1,0:T(8,128)S(1)}, u32[]{:S(2)}, u32[]{:S(2)}) collective-permute-start(f32[2,144,512]{2,1,0:T(8,128)S(1)} %get-tuple-element.65.part_1.b_1), channel_id=1, source_target_pairs={{0,1},{1,2},{2,3},{3,4},{4,5},{5,6},{6,7},{7,8},{8,9},{9,10},{10,1... | collective-permute-start | bytes 1769480 | tf_op jit(solution)/shard_map/ppermute | solution.py:366
  148.7 22.1 %copy-start.22 = (f32[2,144,512]{2,1,0:T(8,128)}, f32[2,144,512]{2,1,0:T(8,128)S(1)}, u32[]{:S(2)}) copy-start(f32[2,144,512]{2,1,0:T(8,128)S(1)} %get-tuple-element.54.part_0.b_0) | copy-start | bytes 1769476
  148.7 22.1 %copy-start.24 = (f32[2,144,512]{2,1,0:T(8,128)}, f32[2,144,512]{2,1,0:T(8,128)S(1)}, u32[]{:S(2)}) copy-start(f32[2,144,512]{2,1,0:T(8,128)S(1)} %get-tuple-element.55.part_1.b_1) | copy-start | bytes 1769476
  148.7 22.1 %collective-permute-start.9 = (f32[2,144,512]{2,1,0:T(8,128)S(1)}, f32[2,144,512]{2,1,0:T(8,128)S(1)}, u32[]{:S(2)}, u32[]{:S(2)}) collective-permute-start(f32[2,144,512]{2,1,0:T(8,128)S(1)} %get-tuple-element.55.part_1.b_1), channel_id=1, source_target_pairs={{0,1},{1,2},{2,3},{3,4},{4,5},{5,6},{6,7},{7,8},{8,9},{9,10},{10,1... | collective-permute-start | bytes 1769480 | tf_op jit(solution)/shard_map/ppermute | solution.py:366
  160.2 2.9 %copy-start.32 = (f32[2,144,512]{2,1,0:T(8,128)}, f32[2,144,512]{2,1,0:T(8,128)S(1)}, u32[]{:S(2)}) copy-start(f32[2,144,512]{2,1,0:T(8,128)S(1)} %collective-permute-done.13.part_2.b_2) | copy-start | bytes 1769476
  161.7 10.6 %copy-start.38 = (f32[4,144,512]{2,1,0:T(8,128)}, f32[4,144,512]{2,1,0:T(8,128)S(1)}, u32[]{:S(2)}) copy-start(f32[4,144,512]{2,1,0:T(8,128)S(1)} %get-tuple-element.69.image_ref) | copy-start | bytes 3538948
  161.7 9.1 %copy-start.20 = (f32[2,144,512]{2,1,0:T(8,128)}, f32[2,144,512]{2,1,0:T(8,128)S(1)}, u32[]{:S(2)}) copy-start(f32[2,144,512]{2,1,0:T(8,128)S(1)} %collective-permute-done.11.part_2.b_2) | copy-start | bytes 1769476
  170.8 20.9 %copy-start.6 = (f32[4,144,512]{2,1,0:T(8,128)S(1)}, f32[4,144,512]{2,1,0:T(8,128)}, u32[]{:S(2)}) copy-start(f32[4,144,512]{2,1,0:T(8,128)} %copy-done.5) | copy-start | bytes 3538948
  170.8 20.9 %copy-start.52 = (f32[8,128]{1,0:T(8,128)S(1)}, f32[8,128]{1,0:T(8,128)}, u32[]{:S(2)}) copy-start(f32[8,128]{1,0:T(8,128)} %total.3.dots_ref.dots_0) | copy-start | bytes 12292
  197.9 4.1 %copy-start.4 = (f32[4,144,512]{2,1,0:T(8,128)S(1)}, f32[4,144,512]{2,1,0:T(8,128)}, u32[]{:S(2)}) copy-start(f32[4,144,512]{2,1,0:T(8,128)} %copy-done.3) | copy-start | bytes 3538948
  197.9 4.1 %copy-start.12 = (f32[2,144,512]{2,1,0:T(8,128)S(1)}, f32[2,144,512]{2,1,0:T(8,128)}, u32[]{:S(2)}) copy-start(f32[2,144,512]{2,1,0:T(8,128)} %copy-done.10) | copy-start | bytes 1769476
  197.9 4.1 %copy-start.17 = (f32[2,144,512]{2,1,0:T(8,128)S(1)}, f32[2,144,512]{2,1,0:T(8,128)}, u32[]{:S(2)}) copy-start(f32[2,144,512]{2,1,0:T(8,128)} %copy-done.16) | copy-start | bytes 1769476
  197.9 4.1 %copy-start.19 = (f32[2,144,512]{2,1,0:T(8,128)S(1)}, f32[2,144,512]{2,1,0:T(8,128)}, u32[]{:S(2)}) copy-start(f32[2,144,512]{2,1,0:T(8,128)} %copy-done.18) | copy-start | bytes 1769476
  197.9 4.1 %copy-start.21 = (f32[2,144,512]{2,1,0:T(8,128)S(1)}, f32[2,144,512]{2,1,0:T(8,128)}, u32[]{:S(2)}) copy-start(f32[2,144,512]{2,1,0:T(8,128)} %copy-done.20) | copy-start | bytes 1769476
  197.9 4.1 %copy-start.37 = (f32[4,144,512]{2,1,0:T(8,128)S(1)}, f32[4,144,512]{2,1,0:T(8,128)}, u32[]{:S(2)}) copy-start(f32[4,144,512]{2,1,0:T(8,128)} %copy-done.36) | copy-start | bytes 3538948
  197.9 4.1 %copy-start.54 = (f32[8,128]{1,0:T(8,128)S(1)}, f32[8,128]{1,0:T(8,128)}, u32[]{:S(2)}) copy-start(f32[8,128]{1,0:T(8,128)} %total.4.dots_1) | copy-start | bytes 12292
  201.0 29.9 %collective-permute-start.14 = (f32[2,4,128,256]{3,2,1,0:T(8,128)}, f32[2,4,128,256]{3,2,1,0:T(8,128)}, u32[]{:S(2)}, u32[]{:S(2)}) collective-permute-start(f32[2,4,128,256]{3,2,1,0:T(8,128)} %get-tuple-element.71), channel_id=1, source_target_pairs={{0,16},{16,0},{1,17},{17,1},{2,18},{18,2},{3,19},{19,3},{4,20},{20... | collective-permute-start | bytes 3145736 | tf_op jit(solution)/shard_map/ppermute | solution.py:380
  202.0 4.4 %copy-start.9 = (f32[2,144,512]{2,1,0:T(8,128)S(1)}, f32[2,144,512]{2,1,0:T(8,128)}, u32[]{:S(2)}) copy-start(f32[2,144,512]{2,1,0:T(8,128)} %copy-done.7) | copy-start | bytes 1769476
  202.1 4.4 %copy-start.23 = (f32[2,144,512]{2,1,0:T(8,128)S(1)}, f32[2,144,512]{2,1,0:T(8,128)}, u32[]{:S(2)}) copy-start(f32[2,144,512]{2,1,0:T(8,128)} %copy-done.22) | copy-start | bytes 1769476
  202.1 4.4 %copy-start.25 = (f32[2,144,512]{2,1,0:T(8,128)S(1)}, f32[2,144,512]{2,1,0:T(8,128)}, u32[]{:S(2)}) copy-start(f32[2,144,512]{2,1,0:T(8,128)} %copy-done.24) | copy-start | bytes 1769476
  206.1 26.7 %collective-permute-start.15 = (f32[2,4,128,256]{3,2,1,0:T(8,128)}, f32[2,4,128,256]{3,2,1,0:T(8,128)}, u32[]{:S(2)}, u32[]{:S(2)}) collective-permute-start(f32[2,4,128,256]{3,2,1,0:T(8,128)} %get-tuple-element.75), channel_id=1, source_target_pairs={{0,16},{16,0},{1,17},{17,1},{2,18},{18,2},{3,19},{19,3},{4,20},{20... | collective-permute-start | bytes 3145736 | tf_op jit(solution)/shard_map/ppermute | solution.py:380
  213.2 22.2 %collective-permute-start.16 = (f32[2,4,128,256]{3,2,1,0:T(8,128)}, f32[2,4,128,256]{3,2,1,0:T(8,128)S(1)}, u32[]{:S(2)}, u32[]{:S(2)}) collective-permute-start(f32[2,4,128,256]{3,2,1,0:T(8,128)} %get-tuple-element.79), channel_id=1, source_target_pairs={{0,16},{16,0},{1,17},{17,1},{2,18},{18,2},{3,19},{19,3},{4,20},{20... | collective-permute-start | bytes 3145736 | tf_op jit(solution)/shard_map/ppermute | solution.py:380
  (29 other events, 29.7 us)
where the time goes:
time: 242 us; the launch traced here: 241 us
  Pallas kernels  115 us (48%)
  waiting for transfers between devices  39.6 us (16%)
  local copies, waits for them, and re-layouts  38 us (16%)
  starting transfers between devices  35.6 us (15%)
  other arithmetic  11.1 us (5%)
    pallas_call x3, Pallas kernels, total_of(): pl.pallas_call(functools.partial(total_kernel, count), out_shape=jax.Shap...  51.7 us
    pallas_call x6, Pallas kernels, solve(): pl.pallas_call(functools.partial(solve_kernel, order), out_shape=(half, h...  41.5 us
    unnamed x120, local copies, waits for them, and re-layouts  26.5 us
    ppermute x3, waiting for transfers between devices, shards(): parts_1.append((lo, hi, lax.ppermute(hi, 'sub', to_right)))  13.8 us
    ppermute x3, waiting for transfers between devices, shards(): parts_0.append((lo, hi, lax.ppermute(lo, 'sub', to_left)))  13.3 us
    ppermute x3, waiting for transfers between devices, shards(): high.append(lax.ppermute(edge, 'sub', to_left))  12.4 us
    pallas_call x6, Pallas kernels, image_of(): pl.pallas_call(functools.partial(image_kernel, order, n), out_shape=(jax....  12.3 us
    ppermute x3, starting transfers between devices, shards(): low = [lax.ppermute(source[n, -1:], 'sub', to_right) for n in range(nrhs)]  10.4 us
  transfers between devices with their start and end apart: 17, of which 5 were waited for; matrix products, arithmetic and copies ran while one was open for 7% of the time, Pallas kernels for 39%

commit v1 on v0

v1 whole, which is shorter than its diff:
```python
import functools

import jax
import jax.numpy as jnp
from jax import lax
from jax.experimental import pallas as pl
from jax.experimental.pallas import tpu as pltpu
from jax.sharding import PartitionSpec as P

SWEEPS = 8
OMEGA = 0.8
ROWS = 8
LANES = 128
RIM = 8
PAD = 8
MESH = pl.DeviceIdType.MESH


def lane(t):
    return slice(t * LANES, (t + 1) * LANES)


def beside_lanes(at, row, t):
    zero = jnp.zeros_like(row[t])
    low = row[t - 1] if t > 0 else zero
    high = row[t + 1] if t + 1 < len(row) else zero
    left = pltpu.roll(jnp.where(at == LANES - 1, low, row[t]), 1, 1)
    right = pltpu.roll(jnp.where(at == 0, high, row[t]), LANES - 1, 1)
    return left + right


def kernel(
    count, rhs, diagonal, sol, res, norms, q, c0, c1, img, dg, sc, e, al, slots, mine,
    load_sem, q_send, q_recv, d_send, d_recv, c_send, c_recv, u_send, u_recv, r_send, r_recv,
    a_send, a_recv, o_local, o_send, o_recv,
):
    colour = lax.axis_index("colour")
    sub = lax.axis_index("sub")
    nrhs, cx, ny, nz = rhs.shape
    span = cx // 2 + 2
    tiles = nz // LANES
    own_rows = ny // 2
    rows = own_rows + RIM
    begin = pl.multiple_of(colour * (own_rows - RIM), ROWS)
    own = pl.multiple_of(colour * RIM, ROWS)
    everyone = 2 * count
    me = colour * count + sub
    has_left = sub > 0
    has_right = sub < count - 1
    left = (colour, sub - 1)
    right = (colour, sub + 1)
    partner = (1 - colour, sub)
    at = lax.broadcasted_iota(jnp.int32, (ROWS, LANES), 1)
    whole = pl.ds(PAD, rows)

    def hbm(t, plane=slice(None)):
        return (plane, pl.ds(begin, rows), lane(t))

    for t in range(tiles):
        pltpu.make_async_copy(
            diagonal.at[hbm(t)], dg.at[1 : cx + 1, t], load_sem.at[nrhs]
        ).start()
    for n in range(nrhs):
        for t in range(tiles):
            pltpu.make_async_copy(
                rhs.at[(n,) + hbm(t)], q.at[n, 1 : cx + 1, t], load_sem.at[n]
            ).start()

    barrier = pltpu.get_barrier_semaphore()

    def peer_of(i):
        other = lax.rem(me + i, everyone)
        return (other // count, lax.rem(other, count))

    def greet(i, carry):
        pl.semaphore_signal(barrier, inc=1, device_id=peer_of(i), device_id_type=MESH)
        return carry

    lax.fori_loop(1, everyone, greet, 0)

    zero = jnp.zeros((ROWS, LANES), jnp.float32)
    for t in range(tiles):
        for edge in (0, PAD + rows):
            for k in range(2):
                for p in range(span):
                    e[k, p, t, edge : edge + ROWS, :] = zero
            for n in range(nrhs):
                for p in range(cx + 2):
                    c0[n, p, t, edge : edge + ROWS, :] = zero
                    c1[n, p, t, edge : edge + ROWS, :] = zero

    def clear(ref, index, offset):
        def body(j, carry):
            r = pl.multiple_of(offset + j * ROWS, ROWS)
            for t in range(tiles):
                ref[index + (t, pl.ds(r, ROWS), slice(None))] = zero
            return carry

        lax.fori_loop(0, rows // ROWS, body, 0)

    @pl.when(jnp.logical_not(has_left))
    def _():
        clear(sc, (0,), 0)
        for n in range(nrhs):
            clear(q, (n, 0), 0)
            clear(c1, (n, 0), PAD)
            clear(c1, (n, 1), PAD)

    @pl.when(jnp.logical_not(has_right))
    def _():
        clear(sc, (cx + 1,), 0)
        for n in range(nrhs):
            clear(q, (n, cx + 1), 0)
            clear(c0, (n, cx), PAD)
            clear(c0, (n, cx + 1), PAD)

    pl.semaphore_wait(barrier, everyone - 1)

    def send(src, dst, send_sem, recv_sem, to):
        return pltpu.make_async_remote_copy(
            src_ref=src, dst_ref=dst, send_sem=send_sem, recv_sem=recv_sem,
            device_id=to, device_id_type=MESH,
        )

    def arrived(ref, sem):
        pltpu.make_async_copy(ref, ref, sem).wait()

    @pl.when(has_right)
    def _():
        for t in range(tiles):
            send(
                diagonal.at[hbm(t, cx - 1)], dg.at[0, t],
                q_send.at[nrhs], q_recv.at[nrhs], right,
            ).start()
        for n in range(nrhs):
            for t in range(tiles):
                send(
                    rhs.at[(n,) + hbm(t, cx - 1)], q.at[n, 0, t],
                    q_send.at[n], q_recv.at[n], right,
                ).start()

    @pl.when(has_left)
    def _():
        for t in range(tiles):
            send(diagonal.at[hbm(t, 0)], dg.at[cx + 1, t], d_send, d_recv, left).start()

    def scale_of(low, high):
        def body(j, carry):
            here = pl.ds(pl.multiple_of(j * ROWS, ROWS), ROWS)
            for p in range(low, high):
                for t in range(tiles):
                    full = 6.0 + dg[p, t, here, :]
                    dg[p, t, here, :] = full
                    sc[p, t, here, :] = OMEGA / full
            return carry

        lax.fori_loop(0, rows // ROWS, body, 0)

    arrived(dg.at[1 : cx + 1], load_sem.at[nrhs])
    scale_of(1, cx + 1)

    @pl.when(has_left)
    def _():
        arrived(dg.at[0], q_recv.at[nrhs])
        scale_of(0, 1)

    def solve(n, base, out):
        def first(j, carry):
            r = pl.multiple_of(j * ROWS, ROWS)
            here = pl.ds(r, ROWS)
            for p in range(span):
                for t in range(tiles):
                    e[0, p, t, pl.ds(r + PAD, ROWS), :] = (
                        sc[base + p, t, here, :] * q[n, base + p, t, here, :]
                    )
            return carry

        lax.fori_loop(0, rows // ROWS, first, 0, unroll=True)

        def sweep(src, write):
            def body(j, carry):
                r = pl.multiple_of(j * ROWS, ROWS)
                here = pl.ds(r, ROWS)
                planes = [
                    [e[src, p, t, pl.ds(r + PAD, ROWS), :] for t in range(tiles)]
                    for p in range(span)
                ]
                for p in range(span):
                    for t in range(tiles):
                        total = e[src, p, t, pl.ds(r + PAD - 1, ROWS), :]
                        total = total + e[src, p, t, pl.ds(r + PAD + 1, ROWS), :]
                        if p > 0:
                            total = total + planes[p - 1][t]
                        if p + 1 < span:
                            total = total + planes[p + 1][t]
                        total = total + beside_lanes(at, planes[p], t)
                        total = total + q[n, base + p, t, here, :]
                        value = (1.0 - OMEGA) * planes[p][t]
                        write(p, t, r, value + sc[base + p, t, here, :] * total)
                return carry

            lax.fori_loop(0, rows // ROWS, body, 0, unroll=True)

        def into(dst):
            def write(p, t, r, value):
                e[dst, p, t, pl.ds(r + PAD, ROWS), :] = value

            return write

        def write_out(p, t, r, value):
            out[n, base + p, t, pl.ds(r + PAD, ROWS), :] = value

        def two(s, carry):
            sweep(0, into(1))
            sweep(1, into(0))
            return carry

        lax.fori_loop(0, (SWEEPS - 2) // 2, two, 0)
        sweep(0, write_out)

    def image(n, c, extra):
        kinds = 5 if extra else 2

        def body(j, carry):
            r = pl.multiple_of(own + j * ROWS, ROWS)
            here = pl.ds(r, ROWS)
            sums = list(carry)
            planes = [
                [c[n, p, t, pl.ds(r + PAD, ROWS), :] for t in range(tiles)]
                for p in range(cx + 2)
            ]
            for p in range(1, cx + 1):
                for t in range(tiles):
                    total = c[n, p, t, pl.ds(r + PAD - 1, ROWS), :]
                    total = total + c[n, p, t, pl.ds(r + PAD + 1, ROWS), :]
                    total = total + planes[p - 1][t] + planes[p + 1][t]
                    total = total + beside_lanes(at, planes[p], t)
                    centre = planes[p][t]
                    value = dg[p, t, here, :] * centre - total
                    img[n, p - 1, t, here, :] = value
                    mine_q = q[n, p, t, here, :]
                    sums[0] = sums[0] + mine_q * centre
                    sums[1] = sums[1] + centre * value
                    if extra:
                        sums[2] = sums[2] + mine_q * mine_q
                        sums[3] = sums[3] + mine_q * value
                        sums[4] = sums[4] + value * value
            return tuple(sums)

        sums = lax.fori_loop(0, own_rows // ROWS, body, (zero,) * kinds, unroll=2)
        first = lax.broadcasted_iota(jnp.int32, (1, LANES), 1)
        row = jnp.zeros((1, LANES), jnp.float32)
        for i, value in enumerate(sums):
            row = jnp.where(first == i, jnp.sum(value), row)
        return row

    def share(k, n, row):
        mine[k, n] = row
        slots[k, n, me] = row

        def tell(i, carry):
            send(
                mine.at[k, n], slots.at[k, n, me], a_send.at[k, n], a_recv.at[k, n], peer_of(i)
            ).start()
            return carry

        lax.fori_loop(1, everyone, tell, 0)

    def totals(k, n):
        arrived(slots.at[k, n, pl.ds(0, everyone - 1)], a_recv.at[k, n])
        row = jnp.sum(slots[k, n], axis=0)
        first = lax.broadcasted_iota(jnp.int32, (1, LANES), 1)

        def pick(i):
            value = jnp.sum(jnp.where(first == i, row, 0.0), axis=1, keepdims=True)
            return jnp.broadcast_to(value, (ROWS, LANES))

        return pick

    edge_rows = pl.ds(PAD + own, own_rows)

    def c0_copies(n):
        return (
            send(
                c0.at[n, 0, :, whole], c0.at[n, cx, :, whole],
                c_send.at[0, n, 0], c_recv.at[0, n, 0], left,
            ),
            send(
                c0.at[n, 1, :, edge_rows], c0.at[n, cx + 1, :, edge_rows],
                c_send.at[0, n, 1], c_recv.at[0, n, 1], left,
            ),
        )

    def c1_copies(n):
        return (
            send(
                c1.at[n, cx + 1, :, whole], c1.at[n, 1, :, whole],
                c_send.at[1, n, 0], c_recv.at[1, n, 0], right,
            ),
            send(
                c1.at[n, cx, :, edge_rows], c1.at[n, 0, :, edge_rows],
                c_send.at[1, n, 1], c_recv.at[1, n, 1], right,
            ),
        )

    def q_copy(n):
        return send(q.at[n, 1], q.at[n, cx + 1], u_send.at[n], u_recv.at[n], left)

    rim_from = pl.multiple_of((1 - colour) * (own_rows - RIM) + colour * RIM, ROWS)
    rim_to = pl.multiple_of(colour * own_rows, ROWS)

    def rim_copy(n):
        return send(
            img.at[n, :, :, pl.ds(rim_from, RIM)], img.at[n, :, :, pl.ds(rim_to, RIM)],
            r_send.at[n], r_recv.at[n], partner,
        )

    def stage_a(n, carry):
        arrived(q.at[n, 1 : cx + 1], load_sem.at[n])

        @pl.when(has_left)
        def _():
            arrived(q.at[n, 0], q_recv.at[n])

        solve(n, 0, c0)

        @pl.when(has_left)
        def _():
            for copy in c0_copies(n):
                copy.start()

        return carry

    lax.fori_loop(0, nrhs, stage_a, 0)

    def stage_b(n, carry):
        @pl.when(n < nrhs)
        def _():
            @pl.when(has_right)
            def _():
                for copy in c0_copies(n):
                    copy.wait_recv()

            row = image(n, c0, False)
            rim_copy(n).start()
            share(0, n, row)

        @pl.when(n > 0)
        def _():
            m = n - 1
            pick = totals(0, m)
            alpha = pick(0) / pick(1)
            al[m] = alpha
            rim_copy(m).wait_recv()

            def body(j, carry):
                here = pl.ds(pl.multiple_of(j * ROWS, ROWS), ROWS)
                for p in range(cx):
                    for t in range(tiles):
                        value = q[m, p + 1, t, here, :] - alpha * img[m, p, t, here, :]
                        q[m, p + 1, t, here, :] = value
                return carry

            lax.fori_loop(0, rows // ROWS, body, 0)

            @pl.when(has_left)
            def _():
                q_copy(m).start()

        return carry

    lax.fori_loop(0, nrhs + 1, stage_b, 0)

    @pl.when(has_right)
    def _():
        arrived(dg.at[cx + 1], d_recv)
        scale_of(cx + 1, cx + 2)

    def stage_c(n, carry):
        @pl.when(has_right)
        def _():
            q_copy(n).wait_recv()

        solve(n, cx // 2, c1)

        @pl.when(has_right)
        def _():
            for copy in c1_copies(n):
                copy.start()

        return carry

    lax.fori_loop(0, nrhs, stage_c, 0)

    half = tiles // 2
    out_rows = pl.ds(pl.multiple_of(colour * own_rows, ROWS), own_rows)
    q_rows = pl.ds(own, own_rows)

    def out_copies(n):
        for t in range(half):
            for src, dst, r in ((c0, sol, edge_rows), (q, res, q_rows)):
                yield (
                    pltpu.make_async_copy(
                        src.at[n, 1 : cx + 1, colour * half + t, r],
                        dst.at[n, :, out_rows, lane(t)],
                        o_local.at[n],
                    ),
                    send(
                        src.at[n, 1 : cx + 1, (1 - colour) * half + t, r],
                        dst.at[n, :, out_rows, lane(t)],
                        o_send.at[n], o_recv.at[n], partner,
                    ),
                )

    def stage_d(n, carry):
        @pl.when(n < nrhs)
        def _():
            @pl.when(has_left)
            def _():
                for copy in c1_copies(n):
                    copy.wait_recv()

            rim_copy(n).wait_send()
            share(1, n, image(n, c1, True))

        @pl.when(n > 0)
        def _():
            m = n - 1

            @pl.when(has_left)
            def _():
                for copy in c0_copies(m):
                    copy.wait_send()
                q_copy(m).wait_send()

            pick = totals(1, m)
            alpha = pick(0) / pick(1)
            start = al[m]

            def body(j, carry):
                r = pl.multiple_of(own + j * ROWS, ROWS)
                here = pl.ds(r, ROWS)
                there = pl.ds(r + PAD, ROWS)
                for p in range(cx):
                    for t in range(tiles):
                        u = start * c0[m, p + 1, t, there, :] + alpha * c1[m, p + 1, t, there, :]
                        c0[m, p + 1, t, there, :] = u
                        value = q[m, p + 1, t, here, :] - alpha * img[m, p, t, here, :]
                        q[m, p + 1, t, here, :] = value
                return carry

            lax.fori_loop(0, own_rows // ROWS, body, 0)
            for local, remote in out_copies(m):
                local.start()
                remote.start()
            square = pick(2) - 2.0 * alpha * pick(3) + alpha * alpha * pick(4)
            norms[m] = jnp.sqrt(jnp.maximum(square, 0.0))

        return carry

    lax.fori_loop(0, nrhs + 1, stage_d, 0)

    @pl.when(has_right)
    def _():
        arrived(dg.at[0], q_send.at[nrhs])
        for n in range(nrhs):
            arrived(q.at[n, 0], q_send.at[n])
            for copy in c1_copies(n):
                copy.wait_send()

    @pl.when(has_left)
    def _():
        arrived(dg.at[cx + 1], d_send)

    for n in range(nrhs):
        for k in range(2):
            arrived(slots.at[k, n, pl.ds(0, everyone - 1)], a_send.at[k, n])
        for sem in (o_local, o_send, o_recv):
            arrived(c0.at[n, 1 : cx + 1, :, edge_rows], sem.at[n])


def shards(rhs, diagonal):
    count = lax.axis_size("sub")
    nrhs, cx, ny, nz = rhs.shape
    assert cx == 4 and SWEEPS % 2 == 0
    tiles = nz // LANES
    rows = ny // 2 + RIM
    padded = rows + 2 * PAD
    f32 = jnp.float32
    out = jax.ShapeDtypeStruct((nrhs, cx, ny, nz // 2), f32)
    dma = pltpu.SemaphoreType.DMA
    anywhere = pl.BlockSpec(memory_space=pl.ANY)
    sol, res, norms = pl.pallas_call(
        functools.partial(kernel, count),
        out_shape=(out, out, jax.ShapeDtypeStruct((nrhs, ROWS, LANES), f32)),
        in_specs=[anywhere, anywhere],
        out_specs=(anywhere, anywhere, pl.BlockSpec(memory_space=pltpu.VMEM)),
        scratch_shapes=[
            pltpu.VMEM((nrhs, cx + 2, tiles, rows, LANES), f32),
            pltpu.VMEM((nrhs, cx + 2, tiles, padded, LANES), f32),
            pltpu.VMEM((nrhs, cx + 2, tiles, padded, LANES), f32),
            pltpu.VMEM((nrhs, cx, tiles, rows, LANES), f32),
            pltpu.VMEM((cx + 2, tiles, rows, LANES), f32),
            pltpu.VMEM((cx + 2, tiles, rows, LANES), f32),
            pltpu.VMEM((2, cx // 2 + 2, tiles, padded, LANES), f32),
            pltpu.VMEM((nrhs, ROWS, LANES), f32),
            pltpu.VMEM((2, nrhs, 2 * count, 1, LANES), f32),
            pltpu.VMEM((2, nrhs, 1, LANES), f32),
            dma((nrhs + 1,)),
            dma((nrhs + 1,)), dma((nrhs + 1,)),
            dma, dma,
            dma((2, nrhs, 2)), dma((2, nrhs, 2)),
            dma((nrhs,)), dma((nrhs,)),
            dma((nrhs,)), dma((nrhs,)),
            dma((2, nrhs)), dma((2, nrhs)),
            dma((nrhs,)), dma((nrhs,)), dma((nrhs,)),
        ],
        compiler_params=pltpu.CompilerParams(
            collective_id=0, has_side_effects=True, vmem_limit_bytes=56 << 20
        ),
        name="schwarz",
    )(rhs, diagonal)
    return sol, res, norms[:, 0, 0]


def solution(mesh):
    placed = (P(None, "sub", None, None), P("sub", None, None))
    return jax.shard_map(
        shards,
        mesh=mesh,
        in_specs=placed,
        out_specs=(P(None, "sub", None, "colour"), P(None, "sub", None, "colour"), P()),
        check_vma=False,
    )
```

time: 242 us -> 181 us (0.75)
  Pallas kernels: 115 us -> 173 us
  waiting for transfers between devices: 39.6 us -> 0 us
  starting transfers between devices: 35.6 us -> 0 us
  local copies, waits for them, and re-layouts: 38 us -> 6.9 us
  other arithmetic: 11.1 us -> 0 us
    pallas_call x21 -> x1, Pallas kernels: 115 us -> 173 us  [shards(): pl.pallas_call(functools.partial(kernel, count), out_shape=(out, out, jax...]
    ppermute x17 -> x0, waiting for transfers between devices: 39.6 us -> none  [the longest x3 13.8 us: shards(): parts_1.append((lo, hi, lax.ppermute(hi, 'sub', to_right)))]
    ppermute x17 -> x0, starting transfers between devices: 35.6 us -> none  [the longest x3 10.4 us: shards(): low = [lax.ppermute(source[n, -1:], 'sub', to_right) for n in range(nrhs)]]
    unnamed x120 -> x4, local copies, waits for them, and re-layouts: 26.5 us -> 5.58 us
    squeeze x2 -> x0, local copies, waits for them, and re-layouts: 5.7 us -> none  [the longest x1 3.58 us: shards(): q = [source[n] for n in range(nrhs)]]
    another operation x2 -> x0, other arithmetic: 3.91 us -> none  [shards(): return (jnp.stack(solved), jnp.stack(left), jnp.sqrt(squares))]
    select_n x3 -> x0, other arithmetic: 3.36 us -> none  [shards(): jnp.where(first, got, kept)]
    slice x2 -> x1, local copies, waits for them, and re-layouts: 4.52 us -> 1.32 us  [shards(): return (sol, res, norms[:, 0, 0])]
  transfers between devices with their start and end apart: 17 -> 0, of which waited for: 5 -> 0; matrix products, arithmetic and copies ran while one was open for 7% -> 0% of each run, Pallas kernels for 39% -> 0%
where the time goes in v1:
time: 181 us
  Pallas kernels  173 us (96%)
  local copies, waits for them, and re-layouts  6.9 us (4%)
    pallas_call x1, Pallas kernels, shards(): pl.pallas_call(functools.partial(kernel, count), out_shape=(out, out, jax...  173 us
    unnamed x4, local copies, waits for them, and re-layouts  5.58 us

profile of v1, /device:TPU:0, one launch (start us, length us, event | category | flops | bytes accessed | tf_op | source)
XLA Modules:
  0.0 181.0 jit_solution(17508355252115724660)
XLA Ops:
  0.6 173.5 %schwarz.1 = (f32[3,4,256,256]{3,2,1,0:T(8,128)}, f32[3,4,256,256]{3,2,1,0:T(8,128)}, f32[3,8,128]{2,1,0:T(8,128)}) custom-call(f32[3,4,256,512]{3,2,1,0:T(8,128)} %rhs.2, f32[4,256,512]{2,1,0:T(8,128)} %diagonal.1), custom_call_target="tpu_custom_call" | custom-call | tf_op jit(solution)/shard_map/schwarz/pallas_call | solution.py:493
  174.1 1.3 slice_reduce_fusion
  175.4 0.0 copy-start
  175.4 3.9 %copy.7 = f32[3,4,256,256]{3,2,1,0:T(8,128)} copy(f32[3,4,256,256]{3,2,1,0:T(8,128)} %get-tuple-element.12) | data formatting | bytes 6291456
  179.4 0.0 copy-done
  179.4 1.7 copy.8
Async XLA Ops:
  175.4 3.9 %copy-start = (f32[3,4,256,256]{3,2,1,0:T(8,128)S(1)}, f32[3,4,256,256]{3,2,1,0:T(8,128)}, u32[]{:S(2)}) copy-start(f32[3,4,256,256]{3,2,1,0:T(8,128)} %get-tuple-element.13) | copy-start | bytes 9437188

commit v2 on v1

--- a/solution.py
+++ b/solution.py
@@ -32,7 +32,7 @@
 def kernel(
     count, rhs, diagonal, sol, res, norms, q, c0, c1, img, dg, sc, e, al, slots, mine,
     load_sem, q_send, q_recv, d_send, d_recv, c_send, c_recv, u_send, u_recv, r_send, r_recv,
-    a_send, a_recv, o_local, o_send, o_recv,
+    a_send, a_recv, o_send, o_recv,
 ):
     colour = lax.axis_index("colour")
     sub = lax.axis_index("sub")
@@ -114,7 +114,8 @@
             clear(c0, (n, cx), PAD)
             clear(c0, (n, cx + 1), PAD)
 
-    pl.semaphore_wait(barrier, everyone - 1)
+    with jax.named_scope("barrier"):
+        pl.semaphore_wait(barrier, everyone - 1)
 
     def send(src, dst, send_sem, recv_sem, to):
         return pltpu.make_async_remote_copy(
@@ -139,11 +140,6 @@
                     q_send.at[n], q_recv.at[n], right,
                 ).start()
 
-    @pl.when(has_left)
-    def _():
-        for t in range(tiles):
-            send(diagonal.at[hbm(t, 0)], dg.at[cx + 1, t], d_send, d_recv, left).start()
-
     def scale_of(low, high):
         def body(j, carry):
             here = pl.ds(pl.multiple_of(j * ROWS, ROWS), ROWS)
@@ -161,8 +157,9 @@
 
     @pl.when(has_left)
     def _():
-        arrived(dg.at[0], q_recv.at[nrhs])
-        scale_of(0, 1)
+        with jax.named_scope("d_wait"):
+            arrived(dg.at[0], q_recv.at[nrhs])
+            scale_of(0, 1)
 
     def solve(n, base, out):
         def first(j, carry):
@@ -175,7 +172,7 @@
                     )
             return carry
 
-        lax.fori_loop(0, rows // ROWS, first, 0, unroll=True)
+        lax.fori_loop(0, rows // ROWS, first, 0)
 
         def sweep(src, write):
             def body(j, carry):
@@ -218,18 +215,16 @@
         lax.fori_loop(0, (SWEEPS - 2) // 2, two, 0)
         sweep(0, write_out)
 
-    def image(n, c, extra):
-        kinds = 5 if extra else 2
-
+    def image(n, c, low, high, sums, extra):
         def body(j, carry):
             r = pl.multiple_of(own + j * ROWS, ROWS)
             here = pl.ds(r, ROWS)
             sums = list(carry)
-            planes = [
-                [c[n, p, t, pl.ds(r + PAD, ROWS), :] for t in range(tiles)]
-                for p in range(cx + 2)
-            ]
-            for p in range(1, cx + 1):
+            planes = {
+                p: [c[n, p, t, pl.ds(r + PAD, ROWS), :] for t in range(tiles)]
+                for p in range(low - 1, high + 1)
+            }
+            for p in range(low, high):
                 for t in range(tiles):
                     total = c[n, p, t, pl.ds(r + PAD - 1, ROWS), :]
                     total = total + c[n, p, t, pl.ds(r + PAD + 1, ROWS), :]
@@ -247,7 +242,9 @@
                         sums[4] = sums[4] + value * value
             return tuple(sums)
 
-        sums = lax.fori_loop(0, own_rows // ROWS, body, (zero,) * kinds, unroll=2)
+        return lax.fori_loop(0, own_rows // ROWS, body, sums, unroll=4)
+
+    def row_of(sums):
         first = lax.broadcasted_iota(jnp.int32, (1, LANES), 1)
         row = jnp.zeros((1, LANES), jnp.float32)
         for i, value in enumerate(sums):
@@ -315,82 +312,118 @@
             r_send.at[n], r_recv.at[n], partner,
         )
 
-    def stage_a(n, carry):
+    def pipeline(solve_one, send_one, look_one, finish_one):
+        def body(k, carry):
+            @pl.when(k < nrhs)
+            def _():
+                solve_one(k)
+
+            @pl.when((k >= 2) & (k < nrhs + 2))
+            def _():
+                look_one(k - 2)
+
+            @pl.when((k >= 2) & (k < nrhs))
+            def _():
+                send_one(k)
+
+            @pl.when(k >= 3)
+            def _():
+                finish_one(k - 3)
+
+            return carry
+
+        lax.fori_loop(0, nrhs + 3, body, 0)
+
+    def first_sends(n, send_one):
+        @pl.when(n == nrhs - 1)
+        def _():
+            for m in range(2):
+                send_one(m)
+
+    def solve_0(n):
         arrived(q.at[n, 1 : cx + 1], load_sem.at[n])
 
         @pl.when(has_left)
         def _():
-            arrived(q.at[n, 0], q_recv.at[n])
-
-        solve(n, 0, c0)
-
+            with jax.named_scope("q_wait"):
+                arrived(q.at[n, 0], q_recv.at[n])
+
+        @pl.when((n == nrhs - 1) & has_left)
+        def _():
+            for t in range(tiles):
+                send(diagonal.at[hbm(t, 0)], dg.at[cx + 1, t], d_send, d_recv, left).start()
+
+        first_sends(n, send_0)
+        with jax.named_scope("solve_0"):
+            solve(n, 0, c0)
+
+    def send_0(n):
         @pl.when(has_left)
         def _():
             for copy in c0_copies(n):
                 copy.start()
 
-        return carry
-
-    lax.fori_loop(0, nrhs, stage_a, 0)
-
-    def stage_b(n, carry):
-        @pl.when(n < nrhs)
-        def _():
-            @pl.when(has_right)
-            def _():
+    def look_0(n):
+        with jax.named_scope("image_0"):
+            sums = image(n, c0, 1, cx - 1, (zero,) * 2, False)
+
+        @pl.when(has_right)
+        def _():
+            with jax.named_scope("c0_wait"):
                 for copy in c0_copies(n):
                     copy.wait_recv()
 
-            row = image(n, c0, False)
+        with jax.named_scope("image_0"):
+            sums = image(n, c0, cx - 1, cx + 1, sums, False)
+            row = row_of(sums)
             rim_copy(n).start()
             share(0, n, row)
 
-        @pl.when(n > 0)
-        def _():
-            m = n - 1
+    def finish_0(m):
+        with jax.named_scope("total_0"):
             pick = totals(0, m)
             alpha = pick(0) / pick(1)
             al[m] = alpha
+        with jax.named_scope("rim_wait"):
             rim_copy(m).wait_recv()
 
-            def body(j, carry):
-                here = pl.ds(pl.multiple_of(j * ROWS, ROWS), ROWS)
-                for p in range(cx):
-                    for t in range(tiles):
-                        value = q[m, p + 1, t, here, :] - alpha * img[m, p, t, here, :]
-                        q[m, p + 1, t, here, :] = value
-                return carry
-
+        def body(j, carry):
+            here = pl.ds(pl.multiple_of(j * ROWS, ROWS), ROWS)
+            for p in range(cx):
+                for t in range(tiles):
+                    value = q[m, p + 1, t, here, :] - alpha * img[m, p, t, here, :]
+                    q[m, p + 1, t, here, :] = value
+            return carry
+
+        with jax.named_scope("update_0"):
             lax.fori_loop(0, rows // ROWS, body, 0)
 
-            @pl.when(has_left)
-            def _():
-                q_copy(m).start()
-
-        return carry
-
-    lax.fori_loop(0, nrhs + 1, stage_b, 0)
+        @pl.when(has_left)
+        def _():
+            q_copy(m).start()
+
+    pipeline(solve_0, send_0, look_0, finish_0)
 
     @pl.when(has_right)
     def _():
         arrived(dg.at[cx + 1], d_recv)
         scale_of(cx + 1, cx + 2)
 
-    def stage_c(n, carry):
+    def solve_1(n):
         @pl.when(has_right)
         def _():
-            q_copy(n).wait_recv()
-
-        solve(n, cx // 2, c1)
-
+            with jax.named_scope("q1_wait"):
+                q_copy(n).wait_recv()
+
+        first_sends(n, send_1)
+        with jax.named_scope("solve_1"):
+            solve(n, cx // 2, c1)
+
+    def send_1(n):
         @pl.when(has_right)
         def _():
             for copy in c1_copies(n):
                 copy.start()
-
-        return carry
-
-    lax.fori_loop(0, nrhs, stage_c, 0)
 
     half = tiles // 2
     out_rows = pl.ds(pl.multiple_of(colour * own_rows, ROWS), own_rows)
@@ -399,84 +432,86 @@
     def out_copies(n):
         for t in range(half):
             for src, dst, r in ((c0, sol, edge_rows), (q, res, q_rows)):
-                yield (
-                    pltpu.make_async_copy(
-                        src.at[n, 1 : cx + 1, colour * half + t, r],
-                        dst.at[n, :, out_rows, lane(t)],
-                        o_local.at[n],
-                    ),
-                    send(
-                        src.at[n, 1 : cx + 1, (1 - colour) * half + t, r],
-                        dst.at[n, :, out_rows, lane(t)],
-                        o_send.at[n], o_recv.at[n], partner,
-                    ),
+                yield send(
+                    src.at[n, 1 : cx + 1, (1 - colour) * half + t, r],
+                    dst.at[n, :, out_rows, lane(t)],
+                    o_send.at[n], o_recv.at[n], partner,
                 )
 
-    def stage_d(n, carry):
-        @pl.when(n < nrhs)
-        def _():
-            @pl.when(has_left)
-            def _():
+    def look_1(n):
+        rim_copy(n).wait_send()
+        with jax.named_scope("image_1"):
+            sums = image(n, c1, 3, cx + 1, (zero,) * 5, True)
+
+        @pl.when(has_left)
+        def _():
+            with jax.named_scope("c1_wait"):
                 for copy in c1_copies(n):
                     copy.wait_recv()
 
-            rim_copy(n).wait_send()
-            share(1, n, image(n, c1, True))
-
-        @pl.when(n > 0)
-        def _():
-            m = n - 1
-
-            @pl.when(has_left)
-            def _():
-                for copy in c0_copies(m):
-                    copy.wait_send()
-                q_copy(m).wait_send()
-
+        with jax.named_scope("image_1"):
+            sums = image(n, c1, 1, 3, sums, True)
+            share(1, n, row_of(sums))
+
+    def finish_1(m):
+        @pl.when(has_left)
+        def _():
+            for copy in c0_copies(m):
+                copy.wait_send()
+            q_copy(m).wait_send()
+
+        with jax.named_scope("total_1"):
             pick = totals(1, m)
             alpha = pick(0) / pick(1)
             start = al[m]
 
-            def body(j, carry):
-                r = pl.multiple_of(own + j * ROWS, ROWS)
-                here = pl.ds(r, ROWS)
-                there = pl.ds(r + PAD, ROWS)
-                for p in range(cx):
-                    for t in range(tiles):
-                        u = start * c0[m, p + 1, t, there, :] + alpha * c1[m, p + 1, t, there, :]
-                        c0[m, p + 1, t, there, :] = u
+        def body(j, carry):
+            r = pl.multiple_of(own + j * ROWS, ROWS)
+            here = pl.ds(r, ROWS)
+            there = pl.ds(r + PAD, ROWS)
+            out = pl.ds(pl.multiple_of(colour * own_rows + j * ROWS, ROWS), ROWS)
+            for p in range(cx):
+                for i in range(half):
+                    for side in (colour, 1 - colour):
+                        t = side * half + i
+                        u = start * c0[m, p + 1, t, there, :]
+                        u = u + alpha * c1[m, p + 1, t, there, :]
                         value = q[m, p + 1, t, here, :] - alpha * img[m, p, t, here, :]
-                        q[m, p + 1, t, here, :] = value
-                return carry
-
+                        if side is colour:
+                            sol[m, p, out, lane(i)] = u
+                            res[m, p, out, lane(i)] = value
+                        else:
+                            c0[m, p + 1, t, there, :] = u
+                            q[m, p + 1, t, here, :] = value
+            return carry
+
+        with jax.named_scope("finish"):
             lax.fori_loop(0, own_rows // ROWS, body, 0)
-            for local, remote in out_copies(m):
-                local.start()
-                remote.start()
-            square = pick(2) - 2.0 * alpha * pick(3) + alpha * alpha * pick(4)
-            norms[m] = jnp.sqrt(jnp.maximum(square, 0.0))
-
-        return carry
-
-    lax.fori_loop(0, nrhs + 1, stage_d, 0)
-
-    @pl.when(has_right)
-    def _():
-        arrived(dg.at[0], q_send.at[nrhs])
+        for copy in out_copies(m):
+            copy.start()
+        square = pick(2) - 2.0 * alpha * pick(3) + alpha * alpha * pick(4)
+        norms[m] = jnp.max(jnp.sqrt(jnp.maximum(square, 0.0)))
+
+    pipeline(solve_1, send_1, look_1, finish_1)
+
+    with jax.named_scope("drain"):
+        @pl.when(has_right)
+        def _():
+            arrived(dg.at[0], q_send.at[nrhs])
+            for n in range(nrhs):
+                arrived(q.at[n, 0], q_send.at[n])
+                for copy in c1_copies(n):
+                    copy.wait_send()
+
+        @pl.when(has_left)
+        def _():
+            arrived(dg.at[cx + 1], d_send)
+
         for n in range(nrhs):
-            arrived(q.at[n, 0], q_send.at[n])
-            for copy in c1_copies(n):
-                copy.wait_send()
-
-    @pl.when(has_left)
-    def _():
-        arrived(dg.at[cx + 1], d_send)
-
-    for n in range(nrhs):
-        for k in range(2):
-            arrived(slots.at[k, n, pl.ds(0, everyone - 1)], a_send.at[k, n])
-        for sem in (o_local, o_send, o_recv):
-            arrived(c0.at[n, 1 : cx + 1, :, edge_rows], sem.at[n])
+            for k in range(2):
+                arrived(slots.at[k, n, pl.ds(0, everyone - 1)], a_send.at[k, n])
+            for sem in (o_send, o_recv):
+                arrived(c0.at[n, 1 : cx + 1, :, edge_rows], sem.at[n])
 
 
 def shards(rhs, diagonal):
@@ -489,12 +524,13 @@
     f32 = jnp.float32
     out = jax.ShapeDtypeStruct((nrhs, cx, ny, nz // 2), f32)
     dma = pltpu.SemaphoreType.DMA
-    anywhere = pl.BlockSpec(memory_space=pl.ANY)
+    remote = pl.BlockSpec(memory_space=pltpu.HBM)
+    near = pl.BlockSpec(memory_space=pltpu.VMEM)
     sol, res, norms = pl.pallas_call(
         functools.partial(kernel, count),
-        out_shape=(out, out, jax.ShapeDtypeStruct((nrhs, ROWS, LANES), f32)),
-        in_specs=[anywhere, anywhere],
-        out_specs=(anywhere, anywhere, pl.BlockSpec(memory_space=pltpu.VMEM)),
+        out_shape=(out, out, jax.ShapeDtypeStruct((nrhs,), f32)),
+        in_specs=[remote, remote],
+        out_specs=(near, near, pl.BlockSpec(memory_space=pltpu.SMEM)),
         scratch_shapes=[
             pltpu.VMEM((nrhs, cx + 2, tiles, rows, LANES), f32),
             pltpu.VMEM((nrhs, cx + 2, tiles, padded, LANES), f32),
@@ -513,14 +549,17 @@
             dma((nrhs,)), dma((nrhs,)),
             dma((nrhs,)), dma((nrhs,)),
             dma((2, nrhs)), dma((2, nrhs)),
-            dma((nrhs,)), dma((nrhs,)), dma((nrhs,)),
+            dma((nrhs,)), dma((nrhs,)),
         ],
         compiler_params=pltpu.CompilerParams(
-            collective_id=0, has_side_effects=True, vmem_limit_bytes=56 << 20
+            collective_id=0, has_side_effects=True, vmem_limit_bytes=44 << 20
         ),
         name="schwarz",
-    )(rhs, diagonal)
-    return sol, res, norms[:, 0, 0]
+    )(
+        pltpu.with_memory_space_constraint(rhs, pltpu.HBM),
+        pltpu.with_memory_space_constraint(diagonal, pltpu.HBM),
+    )
+    return sol, res, norms
 
 
 def solution(mesh):

time: 181 us -> 145 us (0.80)
  Pallas kernels: 173 us -> 140 us
  local copies, waits for them, and re-layouts: 6.9 us -> 3.84 us
    pallas_call x1, Pallas kernels: 173 us -> 140 us  [shards(): pl.pallas_call(functools.partial(kernel, count), out_shape=(out, out, jax...]
    unnamed x4 -> x3, local copies, waits for them, and re-layouts: 5.58 us -> 3.84 us
where the time goes in v2:
time: 145 us
  Pallas kernels  140 us (97%)
  local copies, waits for them, and re-layouts  3.84 us (3%)
    pallas_call x1, Pallas kernels, shards(): pl.pallas_call(functools.partial(kernel, count), out_shape=(out, out, jax...  140 us
    unnamed x3, local copies, waits for them, and re-layouts  3.84 us

profile of v2, /device:TPU:0, one launch (start us, length us, event | category | flops | bytes accessed | tf_op | source)
XLA Modules:
  0.0 144.8 jit_solution(7140254185638796749)
XLA Ops:
  0.6 140.3 %schwarz.1 = (f32[3,4,256,256]{3,2,1,0:T(8,128)S(1)}, f32[3,4,256,256]{3,2,1,0:T(8,128)S(1)}, f32[3]{0:T(128)S(1)}) custom-call(f32[3,4,256,512]{3,2,1,0:T(8,128)} %rhs.1, f32[4,256,512]{2,1,0:T(8,128)} %diagonal.1), custom_call_target="tpu_custom_call" | custom-call | tf_op jit(solution)/shard_map/schwarz/pallas_call | solution.py:529
  140.9 1.7 %copy.8 = f32[3,4,256,256]{3,2,1,0:T(8,128)} copy(f32[3,4,256,256]{3,2,1,0:T(8,128)S(1)} %get-tuple-element.6) | data formatting | bytes 6291456
  142.6 1.7 %copy.9 = f32[3,4,256,256]{3,2,1,0:T(8,128)} copy(f32[3,4,256,256]{3,2,1,0:T(8,128)S(1)} %get-tuple-element.7) | data formatting | bytes 6291456
  144.3 0.5 copy.10

commit v3 on v2

--- a/solution.py
+++ b/solution.py
@@ -31,8 +31,9 @@
 
 def kernel(
     count, rhs, diagonal, sol, res, norms, q, c0, c1, img, dg, sc, e, al, slots, mine,
+    x_c0, x_q, x_c1, x_img, norm_row,
     load_sem, q_send, q_recv, d_send, d_recv, c_send, c_recv, u_send, u_recv, r_send, r_recv,
-    a_send, a_recv, o_send, o_recv,
+    a_send, a_recv, f_send, f_recv, x_send, x_recv,
 ):
     colour = lax.axis_index("colour")
     sub = lax.axis_index("sub")
@@ -53,8 +54,27 @@
     at = lax.broadcasted_iota(jnp.int32, (ROWS, LANES), 1)
     whole = pl.ds(PAD, rows)
 
-    def hbm(t, plane=slice(None)):
-        return (plane, pl.ds(begin, rows), lane(t))
+    core_rows = pl.ds(pl.multiple_of(colour * own_rows, ROWS), own_rows)
+    q_rows = pl.ds(own, own_rows)
+    edge_rows = pl.ds(PAD + own, own_rows)
+
+    def hbm(t):
+        return (slice(None), pl.ds(begin, rows), lane(t))
+
+    barrier = pltpu.get_barrier_semaphore()
+
+    def every_peer(act):
+        for other, first in ((colour, 1), (1 - colour, 0)):
+
+            def body(i, carry):
+                act((other, lax.rem(sub + i, count)))
+                return carry
+
+            lax.fori_loop(first, count, body, 0, unroll=3 if first else 4)
+
+    every_peer(
+        lambda to: pl.semaphore_signal(barrier, inc=1, device_id=to, device_id_type=MESH)
+    )
 
     for t in range(tiles):
         pltpu.make_async_copy(
@@ -65,18 +85,6 @@
             pltpu.make_async_copy(
                 rhs.at[(n,) + hbm(t)], q.at[n, 1 : cx + 1, t], load_sem.at[n]
             ).start()
-
-    barrier = pltpu.get_barrier_semaphore()
-
-    def peer_of(i):
-        other = lax.rem(me + i, everyone)
-        return (other // count, lax.rem(other, count))
-
-    def greet(i, carry):
-        pl.semaphore_signal(barrier, inc=1, device_id=peer_of(i), device_id_type=MESH)
-        return carry
-
-    lax.fori_loop(1, everyone, greet, 0)
 
     zero = jnp.zeros((ROWS, LANES), jnp.float32)
     for t in range(tiles):
@@ -130,15 +138,53 @@
     def _():
         for t in range(tiles):
             send(
-                diagonal.at[hbm(t, cx - 1)], dg.at[0, t],
+                diagonal.at[cx - 1, core_rows, lane(t)], dg.at[0, t, q_rows],
                 q_send.at[nrhs], q_recv.at[nrhs], right,
             ).start()
         for n in range(nrhs):
             for t in range(tiles):
                 send(
-                    rhs.at[(n,) + hbm(t, cx - 1)], q.at[n, 0, t],
+                    rhs.at[n, cx - 1, core_rows, lane(t)], q.at[n, 0, t, q_rows],
                     q_send.at[n], q_recv.at[n], right,
                 ).start()
+
+    rim_from = (1 - colour) * (own_rows - RIM) + colour * RIM
+    rim_to = colour * own_rows
+
+    def rim_copy(ref, pad, send_sem, recv_sem):
+        return send(
+            ref.at[..., pl.ds(pl.multiple_of(rim_from + pad, ROWS), RIM), :],
+            ref.at[..., pl.ds(pl.multiple_of(rim_to + pad, ROWS), RIM), :],
+            send_sem, recv_sem, partner,
+        )
+
+    def img_rim(n):
+        return rim_copy(img.at[n], 0, r_send.at[n], r_recv.at[n])
+
+    def q_rim(n):
+        return rim_copy(q.at[n, 0], 0, f_send.at[2 + n], f_recv.at[2 + n])
+
+    def q1_rim(n):
+        k = 2 + nrhs + n
+        return rim_copy(q.at[n, cx + 1], 0, f_send.at[k], f_recv.at[k])
+
+    def c0_rim(n):
+        k = 2 + 2 * nrhs + n
+        return rim_copy(c0.at[n, cx], PAD, f_send.at[k], f_recv.at[k])
+
+    half = tiles // 2
+    away = pl.ds((1 - colour) * half, half)
+
+    def cross(k, n):
+        src, dst = (
+            (c0.at[n, 1 : cx + 1, away, edge_rows], x_c0.at[n]),
+            (q.at[n, 1 : cx + 1, away, q_rows], x_q.at[n]),
+            (c1.at[n, 2 : cx + 1, away, edge_rows], x_c1.at[n, 1:cx]),
+            (c1.at[n, 1:2, away, edge_rows], x_c1.at[n, 0:1]),
+            (img.at[n, 2:cx, away, q_rows], x_img.at[n, 2:cx]),
+            (img.at[n, 0:2, away, q_rows], x_img.at[n, 0:2]),
+        )[k]
+        return send(src, dst, x_send.at[n, k], x_recv.at[n, k], partner)
 
     def scale_of(low, high):
         def body(j, carry):
@@ -158,7 +204,10 @@
     @pl.when(has_left)
     def _():
         with jax.named_scope("d_wait"):
-            arrived(dg.at[0], q_recv.at[nrhs])
+            arrived(dg.at[0, :, q_rows], q_recv.at[nrhs])
+            copy = rim_copy(dg.at[0], 0, f_send.at[0], f_recv.at[0])
+            copy.start()
+            copy.wait()
             scale_of(0, 1)
 
     def solve(n, base, out):
@@ -237,9 +286,8 @@
                     sums[0] = sums[0] + mine_q * centre
                     sums[1] = sums[1] + centre * value
                     if extra:
-                        sums[2] = sums[2] + mine_q * mine_q
-                        sums[3] = sums[3] + mine_q * value
-                        sums[4] = sums[4] + value * value
+                        sums[2] = sums[2] + mine_q * value
+                        sums[3] = sums[3] + value * value
             return tuple(sums)
 
         return lax.fori_loop(0, own_rows // ROWS, body, sums, unroll=4)
@@ -251,17 +299,50 @@
             row = jnp.where(first == i, jnp.sum(value), row)
         return row
 
+    def squares(n, cross_sum, square_sum):
+        square = jnp.sum(square_sum)
+        fit = jnp.sum(cross_sum) / jnp.where(square > 0.0, square, 1.0)
+
+        def body(j, carry):
+            here = pl.ds(pl.multiple_of(own + j * ROWS, ROWS), ROWS)
+            low, mixed = list(carry[0]), list(carry[1])
+            for p in range(cx):
+                for t in range(tiles):
+                    value = img[n, p, t, here, :]
+                    rest = q[n, p + 1, t, here, :] - fit * value
+                    low[p] = low[p] + rest * rest
+                    mixed[p] = mixed[p] + rest * value
+            return tuple(low), tuple(mixed)
+
+        low, mixed = lax.fori_loop(
+            0, own_rows // ROWS, body, ((zero,) * cx, (zero,) * cx), unroll=2
+        )
+        first = lax.broadcasted_iota(jnp.int32, (1, LANES), 1)
+        row = jnp.zeros((1, LANES), jnp.float32)
+        for i, value in enumerate((fit, jnp.sum(sum(low)), jnp.sum(sum(mixed)), square)):
+            row = jnp.where(first == i, value, row)
+        return row
+
+    def norm_of(n, alpha):
+        arrived(slots.at[2, n, pl.ds(0, everyone - 1)], a_recv.at[2, n])
+        rows_of = slots[2, n]
+        first = lax.broadcasted_iota(jnp.int32, rows_of.shape, 2)
+        fit, low, mixed, square = (
+            jnp.sum(jnp.where(first == i, rows_of, 0.0), axis=2, keepdims=True) for i in range(4)
+        )
+        gap = alpha[0:1, 0:1][None] - fit
+        total = jnp.sum(low + gap * (gap * square - 2.0 * mixed), axis=0)
+        return jnp.sqrt(jnp.maximum(jnp.broadcast_to(total, (1, LANES)), 0.0))
+
     def share(k, n, row):
         mine[k, n] = row
         slots[k, n, me] = row
 
-        def tell(i, carry):
-            send(
-                mine.at[k, n], slots.at[k, n, me], a_send.at[k, n], a_recv.at[k, n], peer_of(i)
+        every_peer(
+            lambda to: send(
+                mine.at[k, n], slots.at[k, n, me], a_send.at[k, n], a_recv.at[k, n], to
             ).start()
-            return carry
-
-        lax.fori_loop(1, everyone, tell, 0)
+        )
 
     def totals(k, n):
         arrived(slots.at[k, n, pl.ds(0, everyone - 1)], a_recv.at[k, n])
@@ -274,12 +355,10 @@
 
         return pick
 
-    edge_rows = pl.ds(PAD + own, own_rows)
-
     def c0_copies(n):
         return (
             send(
-                c0.at[n, 0, :, whole], c0.at[n, cx, :, whole],
+                c0.at[n, 0, :, edge_rows], c0.at[n, cx, :, edge_rows],
                 c_send.at[0, n, 0], c_recv.at[0, n, 0], left,
             ),
             send(
@@ -301,15 +380,8 @@
         )
 
     def q_copy(n):
-        return send(q.at[n, 1], q.at[n, cx + 1], u_send.at[n], u_recv.at[n], left)
-
-    rim_from = pl.multiple_of((1 - colour) * (own_rows - RIM) + colour * RIM, ROWS)
-    rim_to = pl.multiple_of(colour * own_rows, ROWS)
-
-    def rim_copy(n):
         return send(
-            img.at[n, :, :, pl.ds(rim_from, RIM)], img.at[n, :, :, pl.ds(rim_to, RIM)],
-            r_send.at[n], r_recv.at[n], partner,
+            q.at[n, 1, :, q_rows], q.at[n, cx + 1, :, q_rows], u_send.at[n], u_recv.at[n], left
         )
 
     def pipeline(solve_one, send_one, look_one, finish_one):
@@ -334,28 +406,62 @@
 
         lax.fori_loop(0, nrhs + 3, body, 0)
 
-    def first_sends(n, send_one):
-        @pl.when(n == nrhs - 1)
-        def _():
-            for m in range(2):
-                send_one(m)
+    def q_here():
+        for m in range(1, nrhs):
+            arrived(q.at[m, 0, :, q_rows], q_recv.at[m])
 
     def solve_0(n):
         arrived(q.at[n, 1 : cx + 1], load_sem.at[n])
 
+        @pl.when(n == 1)
+        def _():
+            with jax.named_scope("gate_0"):
+
+                @pl.when(has_right)
+                def _():
+                    for m in range(nrhs):
+                        arrived(q.at[m, 0, :, q_rows], q_send.at[m])
+
+                @pl.when(jnp.logical_not(has_right))
+                def _():
+                    q_here()
+
+                @pl.when(has_left)
+                def _():
+                    for t in range(tiles):
+                        send(
+                            diagonal.at[0, core_rows, lane(t)], dg.at[cx + 1, t, q_rows],
+                            d_send, d_recv, left,
+                        ).start()
+
+                send_0(0)
+
+                @pl.when(has_right & has_left)
+                def _():
+                    q_here()
+
+                @pl.when(has_left)
+                def _():
+                    for m in range(1, nrhs):
+                        q_rim(m).start()
+
         @pl.when(has_left)
         def _():
             with jax.named_scope("q_wait"):
-                arrived(q.at[n, 0], q_recv.at[n])
-
-        @pl.when((n == nrhs - 1) & has_left)
-        def _():
-            for t in range(tiles):
-                send(diagonal.at[hbm(t, 0)], dg.at[cx + 1, t], d_send, d_recv, left).start()
-
-        first_sends(n, send_0)
+
+                @pl.when(n == 0)
+                def _():
+                    arrived(q.at[0, 0, :, q_rows], q_recv.at[0])
+                    q_rim(0).start()
+
+                q_rim(n).wait_recv()
+
         with jax.named_scope("solve_0"):
             solve(n, 0, c0)
+
+        @pl.when(n == 1)
+        def _():
+            send_0(1)
 
     def send_0(n):
         @pl.when(has_left)
@@ -372,12 +478,14 @@
             with jax.named_scope("c0_wait"):
                 for copy in c0_copies(n):
                     copy.wait_recv()
+                c0_rim(n).start()
+                c0_rim(n).wait_recv()
 
         with jax.named_scope("image_0"):
             sums = image(n, c0, cx - 1, cx + 1, sums, False)
-            row = row_of(sums)
-            rim_copy(n).start()
-            share(0, n, row)
+            share(0, n, row_of(sums))
+            img_rim(n).start()
+            cross(0, n).start()
 
     def finish_0(m):
         with jax.named_scope("total_0"):
@@ -385,7 +493,7 @@
             alpha = pick(0) / pick(1)
             al[m] = alpha
         with jax.named_scope("rim_wait"):
-            rim_copy(m).wait_recv()
+            img_rim(m).wait_recv()
 
         def body(j, carry):
             here = pl.ds(pl.multiple_of(j * ROWS, ROWS), ROWS)
@@ -402,46 +510,56 @@
         def _():
             q_copy(m).start()
 
+        cross(1, m).start()
+
     pipeline(solve_0, send_0, look_0, finish_0)
 
     @pl.when(has_right)
     def _():
-        arrived(dg.at[cx + 1], d_recv)
+        arrived(dg.at[cx + 1, :, q_rows], d_recv)
+        copy = rim_copy(dg.at[cx + 1], 0, f_send.at[1], f_recv.at[1])
+        copy.start()
+        copy.wait()
         scale_of(cx + 1, cx + 2)
 
     def solve_1(n):
         @pl.when(has_right)
         def _():
             with jax.named_scope("q1_wait"):
-                q_copy(n).wait_recv()
-
-        first_sends(n, send_1)
+                @pl.when(n == 0)
+                def _():
+                    q_copy(0).wait_recv()
+                    q1_rim(0).start()
+
+                @pl.when(n == 1)
+                def _():
+                    for m in range(1, nrhs):
+                        q_copy(m).wait_recv()
+                        q1_rim(m).start()
+                    send_1(0)
+
+                q1_rim(n).wait_recv()
+
         with jax.named_scope("solve_1"):
             solve(n, cx // 2, c1)
 
+        cross(2, n).start()
+
+        @pl.when(n == 1)
+        def _():
+            send_1(1)
+
     def send_1(n):
         @pl.when(has_right)
         def _():
             for copy in c1_copies(n):
                 copy.start()
 
-    half = tiles // 2
-    out_rows = pl.ds(pl.multiple_of(colour * own_rows, ROWS), own_rows)
-    q_rows = pl.ds(own, own_rows)
-
-    def out_copies(n):
-        for t in range(half):
-            for src, dst, r in ((c0, sol, edge_rows), (q, res, q_rows)):
-                yield send(
-                    src.at[n, 1 : cx + 1, (1 - colour) * half + t, r],
-                    dst.at[n, :, out_rows, lane(t)],
-                    o_send.at[n], o_recv.at[n], partner,
-                )
-
     def look_1(n):
-        rim_copy(n).wait_send()
+        img_rim(n).wait_send()
         with jax.named_scope("image_1"):
-            sums = image(n, c1, 3, cx + 1, (zero,) * 5, True)
+            sums = image(n, c1, 3, cx + 1, (zero,) * 4, True)
+            cross(4, n).start()
 
         @pl.when(has_left)
         def _():
@@ -450,68 +568,88 @@
                     copy.wait_recv()
 
         with jax.named_scope("image_1"):
+            cross(3, n).start()
             sums = image(n, c1, 1, 3, sums, True)
-            share(1, n, row_of(sums))
+            share(1, n, row_of(sums[:2]))
+            cross(5, n).start()
+        with jax.named_scope("squares"):
+            share(2, n, squares(n, sums[2], sums[3]))
 
     def finish_1(m):
-        @pl.when(has_left)
-        def _():
-            for copy in c0_copies(m):
-                copy.wait_send()
-            q_copy(m).wait_send()
-
         with jax.named_scope("total_1"):
             pick = totals(1, m)
             alpha = pick(0) / pick(1)
             start = al[m]
+        with jax.named_scope("cross_wait"):
+            for k in range(6):
+                cross(k, m).wait_recv()
 
         def body(j, carry):
             r = pl.multiple_of(own + j * ROWS, ROWS)
             here = pl.ds(r, ROWS)
             there = pl.ds(r + PAD, ROWS)
-            out = pl.ds(pl.multiple_of(colour * own_rows + j * ROWS, ROWS), ROWS)
+            step = pl.ds(pl.multiple_of(j * ROWS, ROWS), ROWS)
+            near = pl.ds(pl.multiple_of(colour * own_rows + j * ROWS, ROWS), ROWS)
+            far = pl.ds(pl.multiple_of((1 - colour) * own_rows + j * ROWS, ROWS), ROWS)
             for p in range(cx):
                 for i in range(half):
-                    for side in (colour, 1 - colour):
-                        t = side * half + i
-                        u = start * c0[m, p + 1, t, there, :]
-                        u = u + alpha * c1[m, p + 1, t, there, :]
-                        value = q[m, p + 1, t, here, :] - alpha * img[m, p, t, here, :]
-                        if side is colour:
-                            sol[m, p, out, lane(i)] = u
-                            res[m, p, out, lane(i)] = value
-                        else:
-                            c0[m, p + 1, t, there, :] = u
-                            q[m, p + 1, t, here, :] = value
+                    t = colour * half + i
+                    u = start * c0[m, p + 1, t, there, :] + alpha * c1[m, p + 1, t, there, :]
+                    sol[m, p, near, lane(i)] = u
+                    value = q[m, p + 1, t, here, :] - alpha * img[m, p, t, here, :]
+                    res[m, p, near, lane(i)] = value
+                    u = start * x_c0[m, p, i, step, :] + alpha * x_c1[m, p, i, step, :]
+                    sol[m, p, far, lane(i)] = u
+                    value = x_q[m, p, i, step, :] - alpha * x_img[m, p, i, step, :]
+                    res[m, p, far, lane(i)] = value
             return carry
 
         with jax.named_scope("finish"):
-            lax.fori_loop(0, own_rows // ROWS, body, 0)
-        for copy in out_copies(m):
-            copy.start()
-        square = pick(2) - 2.0 * alpha * pick(3) + alpha * alpha * pick(4)
-        norms[m] = jnp.max(jnp.sqrt(jnp.maximum(square, 0.0)))
-
+            lax.fori_loop(0, own_rows // ROWS, body, 0, unroll=2)
+        with jax.named_scope("norm"):
+            norm_row[...] = jnp.where(at[0:1] == m, norm_of(m, alpha), norm_row[...])
+
+    norm_row[...] = jnp.zeros((1, LANES), jnp.float32)
     pipeline(solve_1, send_1, look_1, finish_1)
+    norms[...] = norm_row[0, 0:nrhs]
 
     with jax.named_scope("drain"):
+
         @pl.when(has_right)
         def _():
-            arrived(dg.at[0], q_send.at[nrhs])
+            arrived(dg.at[0, :, q_rows], q_send.at[nrhs])
             for n in range(nrhs):
-                arrived(q.at[n, 0], q_send.at[n])
+                q1_rim(n).wait_send()
+                c0_rim(n).wait_send()
                 for copy in c1_copies(n):
                     copy.wait_send()
 
         @pl.when(has_left)
         def _():
-            arrived(dg.at[cx + 1], d_send)
+            arrived(dg.at[cx + 1, :, q_rows], d_send)
+            for n in range(nrhs):
+                q_rim(n).wait_send()
+                q_copy(n).wait_send()
+                for copy in c0_copies(n):
+                    copy.wait_send()
 
         for n in range(nrhs):
-            for k in range(2):
+            for k in range(3):
                 arrived(slots.at[k, n, pl.ds(0, everyone - 1)], a_send.at[k, n])
-            for sem in (o_send, o_recv):
-                arrived(c0.at[n, 1 : cx + 1, :, edge_rows], sem.at[n])
+            for k in range(6):
+                cross(k, n).wait_send()
+
+
+def store_kernel(sol_in, res_in, norms_in, sol, res, norms, sems):
+    copies = []
+    for n in range(sol.shape[0]):
+        for src, dst in ((sol_in, sol), (res_in, res)):
+            copies.append(pltpu.make_async_copy(src.at[n], dst.at[n], sems.at[len(copies)]))
+    copies.append(pltpu.make_async_copy(norms_in, norms, sems.at[len(copies)]))
+    for copy in copies:
+        copy.start()
+    for copy in copies:
+        copy.wait()
 
 
 def shards(rhs, diagonal):
@@ -524,13 +662,14 @@
     f32 = jnp.float32
     out = jax.ShapeDtypeStruct((nrhs, cx, ny, nz // 2), f32)
     dma = pltpu.SemaphoreType.DMA
+    crossed = pltpu.VMEM((nrhs, cx, tiles // 2, ny // 2, LANES), f32)
     remote = pl.BlockSpec(memory_space=pltpu.HBM)
     near = pl.BlockSpec(memory_space=pltpu.VMEM)
     sol, res, norms = pl.pallas_call(
         functools.partial(kernel, count),
         out_shape=(out, out, jax.ShapeDtypeStruct((nrhs,), f32)),
         in_specs=[remote, remote],
-        out_specs=(near, near, pl.BlockSpec(memory_space=pltpu.SMEM)),
+        out_specs=(near, near, near),
         scratch_shapes=[
             pltpu.VMEM((nrhs, cx + 2, tiles, rows, LANES), f32),
             pltpu.VMEM((nrhs, cx + 2, tiles, padded, LANES), f32),
@@ -540,16 +679,19 @@
             pltpu.VMEM((cx + 2, tiles, rows, LANES), f32),
             pltpu.VMEM((2, cx // 2 + 2, tiles, padded, LANES), f32),
             pltpu.VMEM((nrhs, ROWS, LANES), f32),
-            pltpu.VMEM((2, nrhs, 2 * count, 1, LANES), f32),
-            pltpu.VMEM((2, nrhs, 1, LANES), f32),
+            pltpu.VMEM((3, nrhs, 2 * count, 1, LANES), f32),
+            pltpu.VMEM((3, nrhs, 1, LANES), f32),
+            crossed, crossed, crossed, crossed,
+            pltpu.VMEM((1, LANES), f32),
             dma((nrhs + 1,)),
             dma((nrhs + 1,)), dma((nrhs + 1,)),
             dma, dma,
             dma((2, nrhs, 2)), dma((2, nrhs, 2)),
             dma((nrhs,)), dma((nrhs,)),
             dma((nrhs,)), dma((nrhs,)),
-            dma((2, nrhs)), dma((2, nrhs)),
-            dma((nrhs,)), dma((nrhs,)),
+            dma((3, nrhs)), dma((3, nrhs)),
+            dma((2 + 3 * nrhs,)), dma((2 + 3 * nrhs,)),
+            dma((nrhs, 6)), dma((nrhs, 6)),
         ],
         compiler_params=pltpu.CompilerParams(
             collective_id=0, has_side_effects=True, vmem_limit_bytes=44 << 20
@@ -559,7 +701,15 @@
         pltpu.with_memory_space_constraint(rhs, pltpu.HBM),
         pltpu.with_memory_space_constraint(diagonal, pltpu.HBM),
     )
-    return sol, res, norms
+    return pl.pallas_call(
+        store_kernel,
+        out_shape=(out, out, jax.ShapeDtypeStruct((nrhs,), f32)),
+        in_specs=[pl.BlockSpec(memory_space=pl.ANY)] * 3,
+        out_specs=(remote, remote, remote),
+        scratch_shapes=[dma((2 * nrhs + 1,))],
+        compiler_params=pltpu.CompilerParams(vmem_limit_bytes=1 << 20),
+        name="store",
+    )(sol, res, norms)
 
 
 def solution(mesh):

time: 145 us -> 137 us (0.945)
  Pallas kernels: 140 us -> 136 us
  local copies, waits for them, and re-layouts: 3.84 us -> 0 us
    pallas_call x1, Pallas kernels: 140 us -> 134 us  [shards(): pl.pallas_call(functools.partial(kernel, count), out_shape=(out, out, jax...]
    unnamed x3 -> x0, local copies, waits for them, and re-layouts: 3.84 us -> none
    pallas_call x0 -> x1, Pallas kernels: none -> 2.73 us  [shards(): pl.pallas_call(store_kernel, out_shape=(out, out, jax.ShapeDtypeStruct((n...]
where the time goes in v3:
time: 137 us
  Pallas kernels  136 us (99%)
    pallas_call x1, Pallas kernels, shards(): pl.pallas_call(functools.partial(kernel, count), out_shape=(out, out, jax...  134 us

profile of v3, /device:TPU:0, one launch (start us, length us, event | category | flops | bytes accessed | tf_op | source)
XLA Modules:
  0.0 136.9 jit_solution(6484460299532563012)
XLA Ops:
  0.6 133.6 %schwarz.1 = (f32[3,4,256,256]{3,2,1,0:T(8,128)S(1)}, f32[3,4,256,256]{3,2,1,0:T(8,128)S(1)}, f32[3]{0:T(128)S(1)}) custom-call(f32[3,4,256,512]{3,2,1,0:T(8,128)} %rhs.1, f32[4,256,512]{2,1,0:T(8,128)} %diagonal.1), custom_call_target="tpu_custom_call" | custom-call | tf_op jit(solution)/shard_map/schwarz/pallas_call | solution.py:668
  134.2 2.7 %store.1 = (f32[3,4,256,256]{3,2,1,0:T(8,128)}, f32[3,4,256,256]{3,2,1,0:T(8,128)}, f32[3]{0:T(128)}) custom-call(f32[3,4,256,256]{3,2,1,0:T(8,128)S(1)} %get-tuple-element.6.sol_in, f32[3,4,256,256]{3,2,1,0:T(8,128)S(1)} %get-tuple-element.7.res_in, f32[3]{0:T(128)S(1)} %get-tuple-element.8.norms_in), custom_call_target="tpu_custom_call" | custom-call | tf_op jit(solution)/shard_map/store/pallas_call | solution.py:704

commit v4 on v3

--- a/solution.py
+++ b/solution.py
@@ -31,7 +31,7 @@
 
 def kernel(
     count, rhs, diagonal, sol, res, norms, q, c0, c1, img, dg, sc, e, al, slots, mine,
-    x_c0, x_q, x_c1, x_img, norm_row,
+    x_c0, x_q, x_c1, x_img,
     load_sem, q_send, q_recv, d_send, d_recv, c_send, c_recv, u_send, u_recv, r_send, r_recv,
     a_send, a_recv, f_send, f_recv, x_send, x_recv,
 ):
@@ -52,7 +52,6 @@
     right = (colour, sub + 1)
     partner = (1 - colour, sub)
     at = lax.broadcasted_iota(jnp.int32, (ROWS, LANES), 1)
-    whole = pl.ds(PAD, rows)
 
     core_rows = pl.ds(pl.multiple_of(colour * own_rows, ROWS), own_rows)
     q_rows = pl.ds(own, own_rows)
@@ -75,6 +74,9 @@
     every_peer(
         lambda to: pl.semaphore_signal(barrier, inc=1, device_id=to, device_id_type=MESH)
     )
+
+    def arrived(ref, sem):
+        pltpu.make_async_copy(ref, ref, sem).wait()
 
     for t in range(tiles):
         pltpu.make_async_copy(
@@ -117,11 +119,13 @@
     @pl.when(jnp.logical_not(has_right))
     def _():
         clear(sc, (cx + 1,), 0)
+        clear(dg, (cx + 1,), 0)
         for n in range(nrhs):
             clear(q, (n, cx + 1), 0)
             clear(c0, (n, cx), PAD)
             clear(c0, (n, cx + 1), PAD)
 
+    arrived(dg.at[1 : cx + 1], load_sem.at[nrhs])
     with jax.named_scope("barrier"):
         pl.semaphore_wait(barrier, everyone - 1)
 
@@ -131,16 +135,12 @@
             device_id=to, device_id_type=MESH,
         )
 
-    def arrived(ref, sem):
-        pltpu.make_async_copy(ref, ref, sem).wait()
-
     @pl.when(has_right)
     def _():
-        for t in range(tiles):
-            send(
-                diagonal.at[cx - 1, core_rows, lane(t)], dg.at[0, t, q_rows],
-                q_send.at[nrhs], q_recv.at[nrhs], right,
-            ).start()
+        send(
+            dg.at[cx, :, q_rows], dg.at[0, :, q_rows],
+            q_send.at[nrhs], q_recv.at[nrhs], right,
+        ).start()
         for n in range(nrhs):
             for t in range(tiles):
                 send(
@@ -172,6 +172,10 @@
         k = 2 + 2 * nrhs + n
         return rim_copy(c0.at[n, cx], PAD, f_send.at[k], f_recv.at[k])
 
+    def c1_rim(n):
+        k = 2 + 3 * nrhs + n
+        return rim_copy(c1.at[n, 1], PAD, f_send.at[k], f_recv.at[k])
+
     half = tiles // 2
     away = pl.ds((1 - colour) * half, half)
 
@@ -179,26 +183,29 @@
         src, dst = (
             (c0.at[n, 1 : cx + 1, away, edge_rows], x_c0.at[n]),
             (q.at[n, 1 : cx + 1, away, q_rows], x_q.at[n]),
-            (c1.at[n, 2 : cx + 1, away, edge_rows], x_c1.at[n, 1:cx]),
-            (c1.at[n, 1:2, away, edge_rows], x_c1.at[n, 0:1]),
-            (img.at[n, 2:cx, away, q_rows], x_img.at[n, 2:cx]),
-            (img.at[n, 0:2, away, q_rows], x_img.at[n, 0:2]),
+            (c1.at[n, 1 : cx + 1, away, edge_rows], x_c1.at[n]),
+            (img.at[n, 1:cx, away, q_rows], x_img.at[n, 1:cx]),
+            (img.at[n, 0:1, away, q_rows], x_img.at[n, 0:1]),
         )[k]
+        if k == 4:
+            return send(src, dst, r_send.at[n], r_recv.at[n], partner)
+        k = max(k - 1, 0)
         return send(src, dst, x_send.at[n, k], x_recv.at[n, k], partner)
+
+    def cross_done(k, n, sem):
+        ref = (q.at[n, 0:cx, :, q_rows], x_c1.at[n], x_img.at[n, 1:cx])[k]
+        arrived(ref, sem.at[n, k])
 
     def scale_of(low, high):
         def body(j, carry):
             here = pl.ds(pl.multiple_of(j * ROWS, ROWS), ROWS)
             for p in range(low, high):
                 for t in range(tiles):
-                    full = 6.0 + dg[p, t, here, :]
-                    dg[p, t, here, :] = full
-                    sc[p, t, here, :] = OMEGA / full
+                    sc[p, t, here, :] = OMEGA / (6.0 + dg[p, t, here, :])
             return carry
 
         lax.fori_loop(0, rows // ROWS, body, 0)
 
-    arrived(dg.at[1 : cx + 1], load_sem.at[nrhs])
     scale_of(1, cx + 1)
 
     @pl.when(has_left)
@@ -264,7 +271,7 @@
         lax.fori_loop(0, (SWEEPS - 2) // 2, two, 0)
         sweep(0, write_out)
 
-    def image(n, c, low, high, sums, extra):
+    def image(n, c, low, high, sums):
         def body(j, carry):
             r = pl.multiple_of(own + j * ROWS, ROWS)
             here = pl.ds(r, ROWS)
@@ -280,14 +287,11 @@
                     total = total + planes[p - 1][t] + planes[p + 1][t]
                     total = total + beside_lanes(at, planes[p], t)
                     centre = planes[p][t]
-                    value = dg[p, t, here, :] * centre - total
+                    value = (6.0 + dg[p, t, here, :]) * centre - total
                     img[n, p - 1, t, here, :] = value
                     mine_q = q[n, p, t, here, :]
                     sums[0] = sums[0] + mine_q * centre
                     sums[1] = sums[1] + centre * value
-                    if extra:
-                        sums[2] = sums[2] + mine_q * value
-                        sums[3] = sums[3] + value * value
             return tuple(sums)
 
         return lax.fori_loop(0, own_rows // ROWS, body, sums, unroll=4)
@@ -299,40 +303,82 @@
             row = jnp.where(first == i, jnp.sum(value), row)
         return row
 
-    def squares(n, cross_sum, square_sum):
-        square = jnp.sum(square_sum)
-        fit = jnp.sum(cross_sum) / jnp.where(square > 0.0, square, 1.0)
-
+    def block(n):
+        low, high = cx // 2, cx // 2 + span
+
+        def body(j, carry):
+            r = pl.multiple_of(own + j * ROWS, ROWS)
+            here = pl.ds(r, ROWS)
+            upper, lower = list(carry[0]), list(carry[1])
+            planes = {
+                p: [c1[n, p, t, pl.ds(r + PAD, ROWS), :] for t in range(tiles)]
+                for p in range(low, high)
+            }
+            for p in range(low, high):
+                for t in range(tiles):
+                    total = c1[n, p, t, pl.ds(r + PAD - 1, ROWS), :]
+                    total = total + c1[n, p, t, pl.ds(r + PAD + 1, ROWS), :]
+                    if p > low:
+                        total = total + planes[p - 1][t]
+                    if p + 1 < high:
+                        total = total + planes[p + 1][t]
+                    total = total + beside_lanes(at, planes[p], t)
+                    centre = planes[p][t]
+                    value = (6.0 + dg[p, t, here, :]) * centre - total
+                    if p <= cx:
+                        img[n, p - 1, t, here, :] = value
+                    upper[p - low] = upper[p - low] + q[n, p, t, here, :] * centre
+                    lower[p - low] = lower[p - low] + centre * value
+            return tuple(upper), tuple(lower)
+
+        return lax.fori_loop(
+            0, own_rows // ROWS, body, ((zero,) * span, (zero,) * span), unroll=4
+        )
+
+    def couple(n):
+        first = cx // 2
+
+        def body(j, total):
+            r = pl.multiple_of(own + j * ROWS, ROWS)
+            here = pl.ds(r, ROWS)
+            for t in range(tiles):
+                beside = c1[n, first - 1, t, pl.ds(r + PAD, ROWS), :]
+                total = total + beside * c1[n, first, t, pl.ds(r + PAD, ROWS), :]
+                img[n, first - 1, t, here, :] = img[n, first - 1, t, here, :] - beside
+            return total
+
+        return lax.fori_loop(0, own_rows // ROWS, body, zero, unroll=4)
+
+    def edge(n, alpha, total):
+        def body(j, total):
+            r = pl.multiple_of(own + j * ROWS, ROWS)
+            here = pl.ds(r, ROWS)
+            there = pl.ds(r + PAD, ROWS)
+            row = [c1[n, 1, t, there, :] for t in range(tiles)]
+            for t in range(tiles):
+                around = c1[n, 1, t, pl.ds(r + PAD - 1, ROWS), :]
+                around = around + c1[n, 1, t, pl.ds(r + PAD + 1, ROWS), :]
+                around = around + c1[n, 0, t, there, :] + c1[n, 2, t, there, :]
+                around = around + beside_lanes(at, row, t)
+                value = (6.0 + dg[1, t, here, :]) * row[t] - around
+                img[n, 0, t, here, :] = value
+                rest = q[n, 1, t, here, :] - alpha * value
+                total = total + rest * rest
+            return total
+
+        return lax.fori_loop(0, own_rows // ROWS, body, total, unroll=4)
+
+    def squares(n, alpha):
         def body(j, carry):
             here = pl.ds(pl.multiple_of(own + j * ROWS, ROWS), ROWS)
-            low, mixed = list(carry[0]), list(carry[1])
-            for p in range(cx):
+            sums = list(carry)
+            for p in range(1, cx):
                 for t in range(tiles):
-                    value = img[n, p, t, here, :]
-                    rest = q[n, p + 1, t, here, :] - fit * value
-                    low[p] = low[p] + rest * rest
-                    mixed[p] = mixed[p] + rest * value
-            return tuple(low), tuple(mixed)
-
-        low, mixed = lax.fori_loop(
-            0, own_rows // ROWS, body, ((zero,) * cx, (zero,) * cx), unroll=2
-        )
-        first = lax.broadcasted_iota(jnp.int32, (1, LANES), 1)
-        row = jnp.zeros((1, LANES), jnp.float32)
-        for i, value in enumerate((fit, jnp.sum(sum(low)), jnp.sum(sum(mixed)), square)):
-            row = jnp.where(first == i, value, row)
-        return row
-
-    def norm_of(n, alpha):
-        arrived(slots.at[2, n, pl.ds(0, everyone - 1)], a_recv.at[2, n])
-        rows_of = slots[2, n]
-        first = lax.broadcasted_iota(jnp.int32, rows_of.shape, 2)
-        fit, low, mixed, square = (
-            jnp.sum(jnp.where(first == i, rows_of, 0.0), axis=2, keepdims=True) for i in range(4)
-        )
-        gap = alpha[0:1, 0:1][None] - fit
-        total = jnp.sum(low + gap * (gap * square - 2.0 * mixed), axis=0)
-        return jnp.sqrt(jnp.maximum(jnp.broadcast_to(total, (1, LANES)), 0.0))
+                    rest = q[n, p + 1, t, here, :] - alpha * img[n, p, t, here, :]
+                    sums[p - 1] = sums[p - 1] + rest * rest
+            return tuple(sums)
+
+        return sum(lax.fori_loop(0, own_rows // ROWS, body, (zero,) * (cx - 1), unroll=2))
 
     def share(k, n, row):
         mine[k, n] = row
@@ -340,7 +386,7 @@
 
         every_peer(
             lambda to: send(
-                mine.at[k, n], slots.at[k, n, me], a_send.at[k, n], a_recv.at[k, n], to
+                mine.at[k, n], slots.at[k, n, me], a_send, a_recv.at[k, n], to
             ).start()
         )
 
@@ -355,28 +401,16 @@
 
         return pick
 
-    def c0_copies(n):
-        return (
-            send(
-                c0.at[n, 0, :, edge_rows], c0.at[n, cx, :, edge_rows],
-                c_send.at[0, n, 0], c_recv.at[0, n, 0], left,
-            ),
-            send(
-                c0.at[n, 1, :, edge_rows], c0.at[n, cx + 1, :, edge_rows],
-                c_send.at[0, n, 1], c_recv.at[0, n, 1], left,
-            ),
+    def c0_copy(n):
+        return send(
+            c0.at[n, 0:2, :, edge_rows], c0.at[n, cx : cx + 2, :, edge_rows],
+            c_send.at[n, 2], c_recv.at[n, 2], left,
         )
 
-    def c1_copies(n):
-        return (
-            send(
-                c1.at[n, cx + 1, :, whole], c1.at[n, 1, :, whole],
-                c_send.at[1, n, 0], c_recv.at[1, n, 0], right,
-            ),
-            send(
-                c1.at[n, cx, :, edge_rows], c1.at[n, 0, :, edge_rows],
-                c_send.at[1, n, 1], c_recv.at[1, n, 1], right,
-            ),
+    def c1_copy(n, k):
+        return send(
+            c1.at[n, cx + 1 - k, :, edge_rows], c1.at[n, 1 - k, :, edge_rows],
+            c_send.at[n, k], c_recv.at[n, k], right,
         )
 
     def q_copy(n):
@@ -428,11 +462,9 @@
 
                 @pl.when(has_left)
                 def _():
-                    for t in range(tiles):
-                        send(
-                            diagonal.at[0, core_rows, lane(t)], dg.at[cx + 1, t, q_rows],
-                            d_send, d_recv, left,
-                        ).start()
+                    send(
+                        dg.at[1, :, q_rows], dg.at[cx + 1, :, q_rows], d_send, d_recv, left
+                    ).start()
 
                 send_0(0)
 
@@ -466,23 +498,21 @@
     def send_0(n):
         @pl.when(has_left)
         def _():
-            for copy in c0_copies(n):
-                copy.start()
+            c0_copy(n).start()
 
     def look_0(n):
         with jax.named_scope("image_0"):
-            sums = image(n, c0, 1, cx - 1, (zero,) * 2, False)
+            sums = image(n, c0, 1, cx - 1, (zero,) * 2)
 
         @pl.when(has_right)
         def _():
             with jax.named_scope("c0_wait"):
-                for copy in c0_copies(n):
-                    copy.wait_recv()
+                c0_copy(n).wait_recv()
                 c0_rim(n).start()
                 c0_rim(n).wait_recv()
 
         with jax.named_scope("image_0"):
-            sums = image(n, c0, cx - 1, cx + 1, sums, False)
+            sums = image(n, c0, cx - 1, cx + 1, sums)
             share(0, n, row_of(sums))
             img_rim(n).start()
             cross(0, n).start()
@@ -522,10 +552,15 @@
         copy.wait()
         scale_of(cx + 1, cx + 2)
 
-    def solve_1(n):
+    def q1_here():
+        for m in range(1, nrhs):
+            q_copy(m).wait_recv()
+
+    def solve_1(n, carry):
         @pl.when(has_right)
         def _():
             with jax.named_scope("q1_wait"):
+
                 @pl.when(n == 0)
                 def _():
                     q_copy(0).wait_recv()
@@ -533,85 +568,129 @@
 
                 @pl.when(n == 1)
                 def _():
+                    @pl.when(has_left)
+                    def _():
+                        for m in range(nrhs):
+                            q_copy(m).wait_send()
+
+                    @pl.when(jnp.logical_not(has_left))
+                    def _():
+                        q1_here()
+
+                    c1_copy(0, 0).start()
+
+                    @pl.when(has_left)
+                    def _():
+                        q1_here()
+
                     for m in range(1, nrhs):
-                        q_copy(m).wait_recv()
                         q1_rim(m).start()
-                    send_1(0)
 
                 q1_rim(n).wait_recv()
 
         with jax.named_scope("solve_1"):
             solve(n, cx // 2, c1)
 
+        @pl.when((n > 0) & has_right)
+        def _():
+            c1_copy(n, 0).start()
+
+            @pl.when(n == nrhs - 1)
+            def _():
+                c1_copy(0, 1).start()
+
+        return carry
+
+    lax.fori_loop(0, nrhs, solve_1, 0)
+
+    def look_1(n, carry):
+        img_rim(n).wait_send()
+        with jax.named_scope("block"):
+            upper, lower = block(n)
+
+        @pl.when(has_left)
+        def _():
+            with jax.named_scope("c1_wait"):
+                c1_copy(n, 0).wait_recv()
+
+        with jax.named_scope("couple"):
+            both = couple(n)
+            share(1, n, row_of((sum(upper), sum(lower) - 2.0 * both)))
+
+        @pl.when((n == nrhs - 1) & has_right)
+        def _():
+            for m in range(1, nrhs):
+                c1_copy(m, 1).start()
+
+        @pl.when(has_left)
+        def _():
+            c1_rim(n).start()
+
         cross(2, n).start()
-
-        @pl.when(n == 1)
-        def _():
-            send_1(1)
-
-    def send_1(n):
-        @pl.when(has_right)
-        def _():
-            for copy in c1_copies(n):
-                copy.start()
-
-    def look_1(n):
-        img_rim(n).wait_send()
-        with jax.named_scope("image_1"):
-            sums = image(n, c1, 3, cx + 1, (zero,) * 4, True)
-            cross(4, n).start()
-
-        @pl.when(has_left)
-        def _():
-            with jax.named_scope("c1_wait"):
-                for copy in c1_copies(n):
-                    copy.wait_recv()
-
-        with jax.named_scope("image_1"):
-            cross(3, n).start()
-            sums = image(n, c1, 1, 3, sums, True)
-            share(1, n, row_of(sums[:2]))
-            cross(5, n).start()
-        with jax.named_scope("squares"):
-            share(2, n, squares(n, sums[2], sums[3]))
-
-    def finish_1(m):
+        cross(3, n).start()
+        return carry
+
+    lax.fori_loop(0, nrhs, look_1, 0)
+
+    def finish_1(m, carry):
         with jax.named_scope("total_1"):
             pick = totals(1, m)
             alpha = pick(0) / pick(1)
             start = al[m]
         with jax.named_scope("cross_wait"):
-            for k in range(6):
-                cross(k, m).wait_recv()
-
-        def body(j, carry):
-            r = pl.multiple_of(own + j * ROWS, ROWS)
-            here = pl.ds(r, ROWS)
-            there = pl.ds(r + PAD, ROWS)
-            step = pl.ds(pl.multiple_of(j * ROWS, ROWS), ROWS)
-            near = pl.ds(pl.multiple_of(colour * own_rows + j * ROWS, ROWS), ROWS)
-            far = pl.ds(pl.multiple_of((1 - colour) * own_rows + j * ROWS, ROWS), ROWS)
-            for p in range(cx):
+            for k in range(3):
+                cross_done(k, m, x_recv)
+
+        def update(solution_planes, residual_planes):
+            def body(j, carry):
+                r = pl.multiple_of(own + j * ROWS, ROWS)
+                here = pl.ds(r, ROWS)
+                there = pl.ds(r + PAD, ROWS)
+                step = pl.ds(pl.multiple_of(j * ROWS, ROWS), ROWS)
+                near = pl.ds(pl.multiple_of(colour * own_rows + j * ROWS, ROWS), ROWS)
+                far = pl.ds(pl.multiple_of((1 - colour) * own_rows + j * ROWS, ROWS), ROWS)
                 for i in range(half):
                     t = colour * half + i
-                    u = start * c0[m, p + 1, t, there, :] + alpha * c1[m, p + 1, t, there, :]
-                    sol[m, p, near, lane(i)] = u
-                    value = q[m, p + 1, t, here, :] - alpha * img[m, p, t, here, :]
-                    res[m, p, near, lane(i)] = value
-                    u = start * x_c0[m, p, i, step, :] + alpha * x_c1[m, p, i, step, :]
-                    sol[m, p, far, lane(i)] = u
-                    value = x_q[m, p, i, step, :] - alpha * x_img[m, p, i, step, :]
-                    res[m, p, far, lane(i)] = value
-            return carry
+                    for p in solution_planes:
+                        u = start * c0[m, p + 1, t, there, :]
+                        sol[m, p, near, lane(i)] = u + alpha * c1[m, p + 1, t, there, :]
+                        u = start * x_c0[m, p, i, step, :]
+                        sol[m, p, far, lane(i)] = u + alpha * x_c1[m, p, i, step, :]
+                    for p in residual_planes:
+                        value = alpha * img[m, p, t, here, :]
+                        res[m, p, near, lane(i)] = q[m, p + 1, t, here, :] - value
+                        value = alpha * x_img[m, p, i, step, :]
+                        res[m, p, far, lane(i)] = x_q[m, p, i, step, :] - value
+                return carry
+
+            lax.fori_loop(0, own_rows // ROWS, body, 0, unroll=2)
 
         with jax.named_scope("finish"):
-            lax.fori_loop(0, own_rows // ROWS, body, 0, unroll=2)
-        with jax.named_scope("norm"):
-            norm_row[...] = jnp.where(at[0:1] == m, norm_of(m, alpha), norm_row[...])
-
-    norm_row[...] = jnp.zeros((1, LANES), jnp.float32)
-    pipeline(solve_1, send_1, look_1, finish_1)
-    norms[...] = norm_row[0, 0:nrhs]
+            update(range(cx), range(1, cx))
+            total = squares(m, alpha)
+
+        @pl.when(has_left)
+        def _():
+            with jax.named_scope("edge_wait"):
+                c1_rim(m).wait_recv()
+                c1_copy(m, 1).wait_recv()
+
+        with jax.named_scope("edge"):
+            total = edge(m, alpha, total)
+            cross(4, m).start()
+            share(2, m, row_of((total,)))
+            cross(4, m).wait_recv()
+            update((), (0,))
+        return carry
+
+    lax.fori_loop(0, nrhs, finish_1, 0)
+
+    with jax.named_scope("norm"):
+        found = jnp.zeros((1, LANES), jnp.float32)
+        for n in range(nrhs):
+            square = totals(2, n)(0)[0:1]
+            found = jnp.where(at[0:1] == n, jnp.sqrt(square), found)
+        norms[...] = found[0, 0:nrhs]
 
     with jax.named_scope("drain"):
 
@@ -621,23 +700,27 @@
             for n in range(nrhs):
                 q1_rim(n).wait_send()
                 c0_rim(n).wait_send()
-                for copy in c1_copies(n):
-                    copy.wait_send()
+                for k in range(2):
+                    c1_copy(n, k).wait_send()
 
         @pl.when(has_left)
         def _():
             arrived(dg.at[cx + 1, :, q_rows], d_send)
             for n in range(nrhs):
                 q_rim(n).wait_send()
+                c1_rim(n).wait_send()
+                c0_copy(n).wait_send()
+
+        @pl.when(has_left & jnp.logical_not(has_right))
+        def _():
+            for n in range(nrhs):
                 q_copy(n).wait_send()
-                for copy in c0_copies(n):
-                    copy.wait_send()
-
+
+        arrived(slots.at[:, :, pl.ds(0, everyone - 1)], a_send)
         for n in range(nrhs):
             for k in range(3):
-                arrived(slots.at[k, n, pl.ds(0, everyone - 1)], a_send.at[k, n])
-            for k in range(6):
-                cross(k, n).wait_send()
+                cross_done(k, n, x_send)
+            cross(4, n).wait_send()
 
 
 def store_kernel(sol_in, res_in, norms_in, sol, res, norms, sems):
@@ -682,16 +765,15 @@
             pltpu.VMEM((3, nrhs, 2 * count, 1, LANES), f32),
             pltpu.VMEM((3, nrhs, 1, LANES), f32),
             crossed, crossed, crossed, crossed,
-            pltpu.VMEM((1, LANES), f32),
             dma((nrhs + 1,)),
             dma((nrhs + 1,)), dma((nrhs + 1,)),
             dma, dma,
-            dma((2, nrhs, 2)), dma((2, nrhs, 2)),
+            dma((nrhs, 3)), dma((nrhs, 3)),
             dma((nrhs,)), dma((nrhs,)),
             dma((nrhs,)), dma((nrhs,)),
-            dma((3, nrhs)), dma((3, nrhs)),
-            dma((2 + 3 * nrhs,)), dma((2 + 3 * nrhs,)),
-            dma((nrhs, 6)), dma((nrhs, 6)),
+            dma, dma((3, nrhs)),
+            dma((2 + 4 * nrhs,)), dma((2 + 4 * nrhs,)),
+            dma((nrhs, 3)), dma((nrhs, 3)),
         ],
         compiler_params=pltpu.CompilerParams(
             collective_id=0, has_side_effects=True, vmem_limit_bytes=44 << 20

time: 137 us -> 135 us (0.985)
  Pallas kernels: 136 us -> 134 us
    pallas_call x1, Pallas kernels: 134 us -> 131 us  [shards(): pl.pallas_call(functools.partial(kernel, count), out_shape=(out, out, jax...]
where the time goes in v4:
time: 135 us
  Pallas kernels  134 us (99%)
    pallas_call x1, Pallas kernels, shards(): pl.pallas_call(functools.partial(kernel, count), out_shape=(out, out, jax...  131 us
    pallas_call x1, Pallas kernels, shards(): pl.pallas_call(store_kernel, out_shape=(out, out, jax.ShapeDtypeStruct((n...  2.73 us

profile of v4, /device:TPU:0, one launch (start us, length us, event | category | flops | bytes accessed | tf_op | source)
XLA Modules:
  0.0 134.6 jit_solution(243296109102925295)
XLA Ops:
  0.6 131.3 %schwarz.1 = (f32[3,4,256,256]{3,2,1,0:T(8,128)S(1)}, f32[3,4,256,256]{3,2,1,0:T(8,128)S(1)}, f32[3]{0:T(128)S(1)}) custom-call(f32[3,4,256,512]{3,2,1,0:T(8,128)} %rhs.1, f32[4,256,512]{2,1,0:T(8,128)} %diagonal.1), custom_call_target="tpu_custom_call" | custom-call | tf_op jit(solution)/shard_map/schwarz/pallas_call | solution.py:751
  131.9 2.7 %store.1 = (f32[3,4,256,256]{3,2,1,0:T(8,128)}, f32[3,4,256,256]{3,2,1,0:T(8,128)}, f32[3]{0:T(128)}) custom-call(f32[3,4,256,256]{3,2,1,0:T(8,128)S(1)} %get-tuple-element.6.sol_in, f32[3,4,256,256]{3,2,1,0:T(8,128)S(1)} %get-tuple-element.7.res_in, f32[3]{0:T(128)S(1)} %get-tuple-element.8.norms_in), custom_call_target="tpu_custom_call" | custom-call | tf_op jit(solution)/shard_map/store/pallas_call | solution.py:786

commit v5 on v4

--- a/solution.py
+++ b/solution.py
@@ -296,11 +296,11 @@
 
         return lax.fori_loop(0, own_rows // ROWS, body, sums, unroll=4)
 
-    def row_of(sums):
-        first = lax.broadcasted_iota(jnp.int32, (1, LANES), 1)
-        row = jnp.zeros((1, LANES), jnp.float32)
+    def row_of(sums, start=0, row=None):
+        if row is None:
+            row = jnp.zeros((1, LANES), jnp.float32)
         for i, value in enumerate(sums):
-            row = jnp.where(first == i, jnp.sum(value), row)
+            row = jnp.where(first_row == start + i, jnp.sum(value), row)
         return row
 
     def block(n):
@@ -380,23 +380,23 @@
 
         return sum(lax.fori_loop(0, own_rows // ROWS, body, (zero,) * (cx - 1), unroll=2))
 
-    def share(k, n, row):
-        mine[k, n] = row
-        slots[k, n, me] = row
+    second, third = nrhs, nrhs + 1
+    first_row = lax.broadcasted_iota(jnp.int32, (1, LANES), 1)
+
+    def share(k, row):
+        mine[k] = row
+        slots[k, me] = row
 
         every_peer(
-            lambda to: send(
-                mine.at[k, n], slots.at[k, n, me], a_send, a_recv.at[k, n], to
-            ).start()
+            lambda to: send(mine.at[k], slots.at[k, me], a_send, a_recv.at[k], to).start()
         )
 
-    def totals(k, n):
-        arrived(slots.at[k, n, pl.ds(0, everyone - 1)], a_recv.at[k, n])
-        row = jnp.sum(slots[k, n], axis=0)
-        first = lax.broadcasted_iota(jnp.int32, (1, LANES), 1)
+    def totals(k):
+        arrived(slots.at[k, pl.ds(0, everyone - 1)], a_recv.at[k])
+        row = jnp.sum(slots[k], axis=0)
 
         def pick(i):
-            value = jnp.sum(jnp.where(first == i, row, 0.0), axis=1, keepdims=True)
+            value = jnp.sum(jnp.where(first_row == i, row, 0.0), axis=1, keepdims=True)
             return jnp.broadcast_to(value, (ROWS, LANES))
 
         return pick
@@ -513,13 +513,13 @@
 
         with jax.named_scope("image_0"):
             sums = image(n, c0, cx - 1, cx + 1, sums)
-            share(0, n, row_of(sums))
+            share(n, row_of(sums))
             img_rim(n).start()
             cross(0, n).start()
 
     def finish_0(m):
         with jax.named_scope("total_0"):
-            pick = totals(0, m)
+            pick = totals(m)
             alpha = pick(0) / pick(1)
             al[m] = alpha
         with jax.named_scope("rim_wait"):
@@ -603,7 +603,7 @@
 
     lax.fori_loop(0, nrhs, solve_1, 0)
 
-    def look_1(n, carry):
+    def look_1(n, row):
         img_rim(n).wait_send()
         with jax.named_scope("block"):
             upper, lower = block(n)
@@ -615,7 +615,11 @@
 
         with jax.named_scope("couple"):
             both = couple(n)
-            share(1, n, row_of((sum(upper), sum(lower) - 2.0 * both)))
+            row = row_of((sum(upper), sum(lower) - 2.0 * both), 2 * n, row)
+
+            @pl.when(n == nrhs - 1)
+            def _():
+                share(second, row)
 
         @pl.when((n == nrhs - 1) & has_right)
         def _():
@@ -628,15 +632,16 @@
 
         cross(2, n).start()
         cross(3, n).start()
-        return carry
-
-    lax.fori_loop(0, nrhs, look_1, 0)
-
-    def finish_1(m, carry):
-        with jax.named_scope("total_1"):
-            pick = totals(1, m)
-            alpha = pick(0) / pick(1)
-            start = al[m]
+        return row
+
+    blank = jnp.zeros((1, LANES), jnp.float32)
+    lax.fori_loop(0, nrhs, look_1, blank)
+    with jax.named_scope("total_1"):
+        pick_second = totals(second)
+
+    def finish_1(m, row):
+        alpha = pick_second(2 * m) / pick_second(2 * m + 1)
+        start = al[m]
         with jax.named_scope("cross_wait"):
             for k in range(3):
                 cross_done(k, m, x_recv)
@@ -678,18 +683,21 @@
         with jax.named_scope("edge"):
             total = edge(m, alpha, total)
             cross(4, m).start()
-            share(2, m, row_of((total,)))
+            row = row_of((total,), m, row)
+
+            @pl.when(m == nrhs - 1)
+            def _():
+                share(third, row)
+
             cross(4, m).wait_recv()
             update((), (0,))
-        return carry
-
-    lax.fori_loop(0, nrhs, finish_1, 0)
+        return row
+
+    lax.fori_loop(0, nrhs, finish_1, blank)
 
     with jax.named_scope("norm"):
-        found = jnp.zeros((1, LANES), jnp.float32)
-        for n in range(nrhs):
-            square = totals(2, n)(0)[0:1]
-            found = jnp.where(at[0:1] == n, jnp.sqrt(square), found)
+        arrived(slots.at[third, pl.ds(0, everyone - 1)], a_recv.at[third])
+        found = jnp.sqrt(jnp.sum(slots[third], axis=0))
         norms[...] = found[0, 0:nrhs]
 
     with jax.named_scope("drain"):
@@ -716,7 +724,7 @@
             for n in range(nrhs):
                 q_copy(n).wait_send()
 
-        arrived(slots.at[:, :, pl.ds(0, everyone - 1)], a_send)
+        arrived(slots.at[:, pl.ds(0, everyone - 1)], a_send)
         for n in range(nrhs):
             for k in range(3):
                 cross_done(k, n, x_send)
@@ -762,8 +770,8 @@
             pltpu.VMEM((cx + 2, tiles, rows, LANES), f32),
             pltpu.VMEM((2, cx // 2 + 2, tiles, padded, LANES), f32),
             pltpu.VMEM((nrhs, ROWS, LANES), f32),
-            pltpu.VMEM((3, nrhs, 2 * count, 1, LANES), f32),
-            pltpu.VMEM((3, nrhs, 1, LANES), f32),
+            pltpu.VMEM((nrhs + 2, 2 * count, 1, LANES), f32),
+            pltpu.VMEM((nrhs + 2, 1, LANES), f32),
             crossed, crossed, crossed, crossed,
             dma((nrhs + 1,)),
             dma((nrhs + 1,)), dma((nrhs + 1,)),
@@ -771,7 +779,7 @@
             dma((nrhs, 3)), dma((nrhs, 3)),
             dma((nrhs,)), dma((nrhs,)),
             dma((nrhs,)), dma((nrhs,)),
-            dma, dma((3, nrhs)),
+            dma, dma((nrhs + 2,)),
             dma((2 + 4 * nrhs,)), dma((2 + 4 * nrhs,)),
             dma((nrhs, 3)), dma((nrhs, 3)),
         ],

time: 135 us -> 133 us (0.985)
  Pallas kernels: 134 us -> 132 us
    pallas_call x1, Pallas kernels: 131 us -> 130 us  [shards(): pl.pallas_call(functools.partial(kernel, count), out_shape=(out, out, jax...]
where the time goes in v5:
time: 133 us
  Pallas kernels  132 us (99%)
    pallas_call x1, Pallas kernels, shards(): pl.pallas_call(functools.partial(kernel, count), out_shape=(out, out, jax...  130 us
    pallas_call x1, Pallas kernels, shards(): pl.pallas_call(store_kernel, out_shape=(out, out, jax.ShapeDtypeStruct((n...  2.73 us

profile of v5, /device:TPU:0, one launch (start us, length us, event | category | flops | bytes accessed | tf_op | source)
XLA Modules:
  0.0 133.1 jit_solution(4226295420178888414)
XLA Ops:
  0.6 129.8 %schwarz.1 = (f32[3,4,256,256]{3,2,1,0:T(8,128)S(1)}, f32[3,4,256,256]{3,2,1,0:T(8,128)S(1)}, f32[3]{0:T(128)S(1)}) custom-call(f32[3,4,256,512]{3,2,1,0:T(8,128)} %rhs.1, f32[4,256,512]{2,1,0:T(8,128)} %diagonal.1), custom_call_target="tpu_custom_call" | custom-call | tf_op jit(solution)/shard_map/schwarz/pallas_call | solution.py:759
  130.4 2.7 %store.1 = (f32[3,4,256,256]{3,2,1,0:T(8,128)}, f32[3,4,256,256]{3,2,1,0:T(8,128)}, f32[3]{0:T(128)}) custom-call(f32[3,4,256,256]{3,2,1,0:T(8,128)S(1)} %get-tuple-element.6.sol_in, f32[3,4,256,256]{3,2,1,0:T(8,128)S(1)} %get-tuple-element.7.res_in, f32[3]{0:T(128)S(1)} %get-tuple-element.8.norms_in), custom_call_target="tpu_custom_call" | custom-call | tf_op jit(solution)/shard_map/store/pallas_call | solution.py:794
